TPU v7x, 32 devices: a whole 2x2x4 slice. The times are simulated.
32 devices in a mesh: row: 8 (over z, core), col: 4 (over y, x).
Axes of the slice: x: 2, y: 2, z: 4, core: 2. Of those that a mesh axis runs over, the one named last changes fastest.
Arguments:
- psi: bfloat16 [1024, 4096], P(('row', 'col')), may hold values from -6 to 6
- hpsi: bfloat16 [1024, 4096], P(('row', 'col')), may hold values from -0.1875 to 0.1875
- eigvec: bfloat16 [4, 8, 128, 8, 4, 128], P(None, 'row', None, None, 'col'), may hold values from -0.09375 to 0.09375
Outputs:
- correlation_tiles: float32 [4, 8, 128, 8, 4, 128], P(None, 'row', None, None, 'col')
- updated_tiles: float32 [4, 8, 128, 8, 4, 128], P(None, 'row', None, None, 'col')
- diag_part: float32 [16], replicated
- offdiag_part: float32 [16], replicated
- rotated: bfloat16 [1024, 8, 4, 128], P('row', None, 'col')
All inputs are finite; a program needn't handle non-finite values.
Results may differ from a plain program's by a relative error of at most 0.001.
Values may be sent and summed in bfloat16 or wider, within the bound.
A program may use at most 128 MiB of HBM per device.

v0:
```python
import functools

import jax
import jax.numpy as jnp
from jax import lax
from jax.experimental import pallas as pl
from jax.experimental.pallas import tpu as pltpu
from jax.sharding import PartitionSpec as P

PB = 16


def inner(left, right):
    return lax.dot_general(
        left, right, (((0,), (0,)), ((), ())), preferred_element_type=jnp.float32
    )


def total(array):
    return jnp.sum(array, axis=(0, 1), keepdims=True)


def panel_kernel(
    sizes, block, lead, vecs, images, diagonal, offdiag,
    panel, places, vector_now, folded, part, full,
    lead_part, lead_piece, lead_all, col_send, col_recv, row_send, row_recv,
    all_send, all_recv,
):
    row_count, col_count, row_tiles, col_tiles, tile = sizes
    row_id = lax.axis_index("row")
    col_id = lax.axis_index("col")

    def col_peer(distance):
        return (row_id, lax.rem(col_id + distance, col_count))

    def row_peer(distance):
        return (lax.rem(row_id + distance, row_count), col_id)

    devices = row_count * col_count
    flat_id = row_id * col_count + col_id

    def any_peer(distance):
        flat = lax.rem(flat_id + distance, devices)
        return (lax.div(flat, col_count), lax.rem(flat, col_count))

    barrier = pltpu.get_barrier_semaphore()
    for distance in range(1, devices):
        pl.semaphore_signal(
            barrier, inc=1, device_id=any_peer(distance), device_id_type=pl.DeviceIdType.MESH
        )
    pl.semaphore_wait(barrier, devices - 1)

    def all_copies(place, slot):
        return [
            pltpu.make_async_remote_copy(
                src_ref=place,
                dst_ref=place,
                send_sem=all_send.at[slot, distance],
                recv_sem=all_recv.at[slot, distance],
                device_id=any_peer(distance),
                device_id_type=pl.DeviceIdType.MESH,
            )
            for distance in range(1, devices)
        ]

    def col_copies(source, target):
        return [
            pltpu.make_async_remote_copy(
                src_ref=source,
                dst_ref=target,
                send_sem=col_send.at[distance],
                recv_sem=col_recv.at[distance],
                device_id=col_peer(distance),
                device_id_type=pl.DeviceIdType.MESH,
            )
            for distance in range(1, col_count)
        ]

    def row_copies(source, target):
        return [
            pltpu.make_async_remote_copy(
                src_ref=source,
                dst_ref=target,
                send_sem=row_send.at[distance],
                recv_sem=row_recv.at[distance],
                device_id=row_peer(distance),
                device_id_type=pl.DeviceIdType.MESH,
            )
            for distance in range(1, row_count)
        ]

    copies = col_copies(lead, lead_part.at[col_id])
    for copy in copies:
        copy.start()
    lead_part[pl.ds(col_id, 1)] = lead[...][None]
    vecs[...] = jnp.zeros_like(vecs)
    images[...] = jnp.zeros_like(images)
    diagonal[...] = jnp.zeros_like(diagonal)
    offdiag[...] = jnp.zeros_like(offdiag)
    lanes = lax.broadcasted_iota(jnp.int32, (row_tiles, tile), 1)
    tiles = lax.broadcasted_iota(jnp.int32, (row_tiles, tile), 0)
    for owner in range(row_count):
        places[owner * row_tiles : (owner + 1) * row_tiles, :] = (
            tiles * row_count + owner
        ) * tile + lanes
    for copy in copies:
        copy.wait()
    summed = lead_part[0]
    for source in range(1, col_count):
        summed = summed + lead_part[source]
    lead_piece[...] = summed
    copies = row_copies(lead_piece, lead_all.at[row_id])
    for copy in copies:
        copy.start()
    lead_all[pl.ds(row_id, 1)] = summed[None]
    for copy in copies:
        copy.wait()
    for owner in range(row_count):
        panel[:, owner * row_tiles : (owner + 1) * row_tiles, :] = lead_all[owner]

    pos = places[...]
    lane = lax.broadcasted_iota(jnp.int32, (1, tile), 1)
    lane3 = lax.broadcasted_iota(jnp.int32, (PB, 1, tile), 2)
    chunk = 64
    rows = row_tiles * tile

    @pl.loop(0, PB)
    def _(step):
        slot = lax.rem(step, 2)
        head_v = jnp.sum(jnp.where(lane3 == step, vecs[:, 0:1, :], 0.0), axis=2, keepdims=True)
        head_w = jnp.sum(jnp.where(lane3 == step, images[:, 0:1, :], 0.0), axis=2, keepdims=True)
        column = panel[step]
        for k in range(PB - 1):
            column = column - vecs[k] * head_w[k] - images[k] * head_v[k]
        below = pos > step + 1
        pivot = total(jnp.where(pos == step + 1, column, 0.0))
        here = total(jnp.where(pos == step, column, 0.0))
        tail = total(jnp.where(below, column * column, 0.0))
        length = jnp.sqrt(pivot * pivot + tail)
        beta = jnp.where(pivot >= 0.0, -length, length)
        tau = (beta - pivot) / beta
        vector = jnp.where(
            pos == step + 1, 1.0, jnp.where(below, column / (pivot - beta), 0.0)
        )
        vector_now[...] = vector
        local = []
        for g in range(col_tiles):
            b = col_id + col_count * g
            local.append(
                vector_now[pl.ds(lax.rem(b, row_count) * row_tiles + lax.div(b, row_count), 1), :]
            )
        for start in range(0, rows, chunk):
            acc = block[start : start + chunk, 0:tile] * local[0]
            for g in range(1, col_tiles):
                acc = acc + block[start : start + chunk, g * tile : (g + 1) * tile] * local[g]
            folded[start : start + chunk, :] = acc
        sums = lax.dot_general(
            jnp.ones((8, tile), jnp.float32),
            folded[...],
            (((1,), (1,)), ((), ())),
            precision=lax.Precision.HIGHEST,
            preferred_element_type=jnp.float32,
        )
        for t in range(row_tiles):
            part[step, row_id, col_id, t : t + 1, :] = sums[0:1, t * tile : (t + 1) * tile]
        sent = all_copies(part.at[step, row_id, col_id], slot)
        for copy in sent:
            copy.start()
        onto_w = [total(images[k] * vector) for k in range(PB - 1)]
        onto_v = [total(vecs[k] * vector) for k in range(PB - 1)]
        fix = vecs[0] * onto_w[0] + images[0] * onto_v[0]
        for k in range(1, PB - 1):
            fix = fix + vecs[k] * onto_w[k] + images[k] * onto_v[k]
        vecs[pl.ds(step, 1)] = vector[None]
        diagonal[...] = jnp.where(lane == step, here, diagonal[...])
        offdiag[...] = jnp.where(lane == step, beta, offdiag[...])
        for copy in sent:
            copy.wait()
        for owner in range(row_count):
            piece = part[step, owner, 0]
            for source in range(1, col_count):
                piece = piece + part[step, owner, source]
            full[owner * row_tiles : (owner + 1) * row_tiles, :] = piece
        image = tau * (full[...] - fix)
        image = image - 0.5 * tau * total(image * vector) * vector
        images[pl.ds(step, 1)] = image[None]


def reduce_panel(block, lead, sizes):
    row_count, col_count, row_tiles, col_tiles, tile = sizes
    all_tiles = row_count * row_tiles
    f32 = jnp.float32
    whole = pl.BlockSpec(memory_space=pltpu.VMEM)
    return pl.pallas_call(
        functools.partial(panel_kernel, sizes),
        out_shape=(
            jax.ShapeDtypeStruct((PB, all_tiles, tile), f32),
            jax.ShapeDtypeStruct((PB, all_tiles, tile), f32),
            jax.ShapeDtypeStruct((1, tile), f32),
            jax.ShapeDtypeStruct((1, tile), f32),
        ),
        in_specs=[whole, whole],
        out_specs=(whole, whole, whole, whole),
        scratch_shapes=[
            pltpu.VMEM((PB, all_tiles, tile), f32),
            pltpu.VMEM((all_tiles, tile), jnp.int32),
            pltpu.VMEM((all_tiles, tile), f32),
            pltpu.VMEM((row_tiles * tile, tile), f32),
            pltpu.VMEM((PB, row_count, col_count, row_tiles, tile), f32),
            pltpu.VMEM((all_tiles, tile), f32),
            pltpu.VMEM((col_count, PB, row_tiles, tile), f32),
            pltpu.VMEM((PB, row_tiles, tile), f32),
            pltpu.VMEM((row_count, PB, row_tiles, tile), f32),
            pltpu.SemaphoreType.DMA((col_count,)),
            pltpu.SemaphoreType.DMA((col_count,)),
            pltpu.SemaphoreType.DMA((row_count,)),
            pltpu.SemaphoreType.DMA((row_count,)),
            pltpu.SemaphoreType.DMA((2, row_count * col_count)),
            pltpu.SemaphoreType.DMA((2, row_count * col_count)),
        ],
        compiler_params=pltpu.CompilerParams(
            collective_id=0, has_side_effects=True, vmem_limit_bytes=24 * 1024 * 1024
        ),
        cost_estimate=pl.CostEstimate(
            flops=400_000_000, bytes_accessed=4_000_000, transcendentals=0
        ),
        name="panel",
    )(block, lead)


def spread_kernel(
    row_count, col_count, rows_in, cols_in, row_all, col_all,
    own_sem, a1_send, a1_recv, a2_send, a2_recv, b1_send, b1_recv,
    right_send, right_recv, left_send, left_recv, pair_send, pair_recv,
):
    row_id = lax.axis_index("row")
    col_id = lax.axis_index("col")
    ring = row_count // 2
    half = ring // 2

    def row_at(shift):
        return lax.rem(row_id + shift + row_count, row_count)

    def col_peer(distance):
        return (row_id, lax.rem(col_id + distance, col_count))

    barrier = pltpu.get_barrier_semaphore()
    for distance in range(1, col_count):
        pl.semaphore_signal(
            barrier, inc=1, device_id=col_peer(distance), device_id_type=pl.DeviceIdType.MESH
        )
    for distance in range(1, row_count):
        pl.semaphore_signal(
            barrier, inc=1, device_id=(row_at(distance), col_id),
            device_id_type=pl.DeviceIdType.MESH,
        )
    pl.semaphore_wait(barrier, row_count + col_count - 2)

    def remote(source, target, send, recv, device):
        return pltpu.make_async_remote_copy(
            src_ref=source, dst_ref=target, send_sem=send, recv_sem=recv,
            device_id=device, device_id_type=pl.DeviceIdType.MESH,
        )

    own = [
        pltpu.make_async_copy(cols_in.at[col_id], col_all.at[:, row_id, col_id], own_sem.at[0]),
        pltpu.make_async_copy(rows_in.at[row_id], row_all.at[:, row_id, col_id], own_sem.at[1]),
    ]
    b1 = []
    for d in range(1, col_count):
        peer = col_peer(d)
        b1.append(remote(
            cols_in.at[peer[1]], col_all.at[:, row_id, col_id], b1_send.at[d], b1_recv.at[d], peer
        ))
    a1 = []
    for d in range(1, row_count):
        peer = row_at(d)
        a1.append(remote(
            rows_in.at[peer], row_all.at[:, row_id, col_id], a1_send.at[d], a1_recv.at[d],
            (peer, col_id),
        ))
    for copy in b1 + own + a1:
        copy.start()
    own[0].wait()
    for copy in b1:
        copy.wait()

    def forward(step, origin, shift, final_part, send, recv):
        place = col_all.at[:, origin] if step < half else col_all.at[final_part, origin]
        return remote(place, place, send.at[step], recv.at[step], (row_at(shift), col_id))

    partner = row_id + 1 - 2 * lax.rem(row_id, 2)

    def to_partner(index, origin):
        place = col_all.at[:, origin]
        return remote(place, place, pair_send.at[index], pair_recv.at[index], (partner, col_id))

    right = [forward(1, row_id, 2, 0, right_send, right_recv)]
    left = [forward(1, row_id, -2, 1, left_send, left_recv)]
    pairs = [to_partner(0, row_id)]
    right[0].start()
    left[0].start()
    pairs[0].start()
    own[1].wait()
    for copy in a1:
        copy.wait()
    a2 = []
    for d in range(1, col_count):
        place = row_all.at[:, :, col_id]
        a2.append(remote(place, place, a2_send.at[d], a2_recv.at[d], col_peer(d)))
        a2[-1].start()
    for step in range(1, half):
        from_left = row_at(-2 * step)
        from_right = row_at(2 * step)
        right[-1].wait_recv()
        right.append(forward(step + 1, from_left, 2, 0, right_send, right_recv))
        right[-1].start()
        left[-1].wait_recv()
        left.append(forward(step + 1, from_right, -2, 1, left_send, left_recv))
        left[-1].start()
        for index, origin in ((2 * step - 1, from_left), (2 * step, from_right)):
            pairs.append(to_partner(index, origin))
            pairs[-1].start()
    right[-1].wait_recv()
    left[-1].wait_recv()
    pairs.append(to_partner(ring - 1, row_at(2 * half)))
    pairs[-1].start()
    for copy in a2:
        copy.wait()
    for copy in pairs:
        copy.wait()
    for copy in right + left:
        copy.wait_send()


def spread(psi, hpsi, row_count, col_count, row_tiles, col_tiles, tile):
    g_rows = psi.shape[0]
    both = jnp.stack([psi, hpsi])
    rows_in = jnp.transpose(
        both.reshape(2, g_rows, row_tiles, row_count, tile), (3, 0, 1, 2, 4)
    ).reshape(row_count, 2, g_rows, row_tiles * tile)
    cols_in = jnp.transpose(
        both.reshape(2, g_rows, col_tiles, col_count, tile), (3, 0, 1, 2, 4)
    ).reshape(col_count, 2, g_rows, col_tiles * tile)
    whole = pl.BlockSpec(memory_space=pltpu.VMEM)
    hbm = pl.BlockSpec(memory_space=pltpu.VMEM)
    ring = row_count // 2
    dma = pltpu.SemaphoreType.DMA
    return pl.pallas_call(
        functools.partial(spread_kernel, row_count, col_count),
        out_shape=(
            jax.ShapeDtypeStruct(
                (2, row_count, col_count, g_rows, row_tiles * tile), psi.dtype
            ),
            jax.ShapeDtypeStruct(
                (2, row_count, col_count, g_rows, col_tiles * tile), psi.dtype
            ),
        ),
        in_specs=[whole, whole],
        out_specs=(hbm, hbm),
        scratch_shapes=[
            dma((2,)),
            dma((row_count,)), dma((row_count,)),
            dma((col_count,)), dma((col_count,)),
            dma((col_count,)), dma((col_count,)),
            dma((ring,)), dma((ring,)), dma((ring,)), dma((ring,)),
            dma((ring,)), dma((ring,)),
        ],
        compiler_params=pltpu.CompilerParams(
            collective_id=1, has_side_effects=True, vmem_limit_bytes=40 * 1024 * 1024
        ),
        cost_estimate=pl.CostEstimate(
            flops=100_000_000, bytes_accessed=8_000_000, transcendentals=0
        ),
        name="spread",
    )(rows_in, cols_in)


def on_device(psi, hpsi, eigvec):
    highest = lax.Precision.HIGHEST
    g_rows = psi.shape[0]
    bands = psi.shape[1]
    row_tiles = eigvec.shape[0]
    tile_size = eigvec.shape[2]
    col_tiles = eigvec.shape[3]
    row_count = lax.axis_size("row")
    col_count = lax.axis_size("col")
    row_id = lax.axis_index("row")
    col_id = lax.axis_index("col")
    gvecs = g_rows * row_count * col_count
    row_width = row_tiles * tile_size
    col_width = col_tiles * tile_size
    row_all, col_all = spread(
        psi, hpsi, row_count, col_count, row_tiles, col_tiles, tile_size
    )
    psi_rows = row_all[0].reshape(gvecs, row_width)
    hpsi_rows = row_all[1].reshape(gvecs, row_width)
    psi_cols = col_all[0].reshape(gvecs, col_width)
    hpsi_cols = col_all[1].reshape(gvecs, col_width)
    reduced = 0.5 * (inner(psi_rows, hpsi_cols) + inner(hpsi_rows, psi_cols))
    correlation = inner(psi_rows, psi_cols) / float(gvecs)
    blocks = reduced.reshape(row_tiles, tile_size, col_tiles, tile_size)
    leading = blocks[:, :, 0, :PB]
    lead = jnp.where(col_id == 0, jnp.transpose(leading, (2, 0, 1)), 0.0)
    sizes = (row_count, col_count, row_tiles, col_tiles, tile_size)
    vecs, images, diagonal, offdiag = reduce_panel(reduced, lead, sizes)
    diagonal = diagonal[0, :PB]
    offdiag = offdiag[0, :PB]

    def rows_of(matrix):
        return lax.dynamic_index_in_dim(
            matrix.reshape(PB, row_count, row_tiles, tile_size), row_id, 1, keepdims=False
        ).reshape(PB, row_width)

    def cols_of(matrix):
        ordered = jnp.transpose(
            matrix.reshape(PB, row_count, row_tiles, tile_size), (0, 2, 1, 3)
        )
        return lax.dynamic_index_in_dim(
            ordered.reshape(PB, col_tiles, col_count, tile_size), col_id, 2, keepdims=False
        ).reshape(PB, col_width)

    left = jnp.concatenate([rows_of(vecs), rows_of(images)], axis=0)
    right = jnp.concatenate([cols_of(images), cols_of(vecs)], axis=0)
    updated = reduced - lax.dot_general(
        left, right, (((0,), (0,)), ((), ())), precision=highest,
        preferred_element_type=jnp.float32,
    )
    flat = eigvec.reshape(row_width, col_width)
    rotated = lax.psum_scatter(
        jnp.dot(psi_rows, flat, preferred_element_type=jnp.float32),
        "row",
        scatter_dimension=0,
        tiled=True,
    )
    tile_shape = (row_tiles, 1, tile_size, col_tiles, 1, tile_size)
    return (
        correlation.reshape(tile_shape),
        updated.reshape(tile_shape),
        diagonal,
        offdiag,
        rotated.astype(jnp.bfloat16).reshape(rotated.shape[0], col_tiles, 1, tile_size),
    )


def solution(mesh):
    return jax.shard_map(
        on_device,
        mesh=mesh,
        in_specs=(
            P(("row", "col"), None),
            P(("row", "col"), None),
            P(None, "row", None, None, "col", None),
        ),
        out_specs=(
            P(None, "row", None, None, "col", None),
            P(None, "row", None, None, "col", None),
            P(),
            P(),
            P("row", None, "col", None),
        ),
        check_vma=False,
    )
```

profile of v0, /device:TPU:0, one launch (start us, length us, event | category | flops | bytes accessed | tf_op | source)
XLA Modules:
  0.0 206.6 jit_solution(6574564438319515929)
XLA Ops:
  7.2 0.0 copy-start.3
  7.2 0.0 reduce-scatter.2.cloned.1.call-start
  7.2 1.2 stack.19
  8.4 1.0 copy.44
  9.4 0.1 copy.27
  9.5 1.1 stack.18
  10.6 0.0 copy-done.3
  10.7 0.1 copy.26
  10.8 0.3 maximum_bitcast_fusion
  11.1 0.2 reshape.88.rows_in
  11.4 0.1 maximum_bitcast_fusion.1
  11.5 0.2 reshape.89.cols_in
  11.7 0.0 copy-start.4
  11.7 54.6 %spread.1 = (bf16[2,8,4,32,512]{4,3,2,1,0:T(8,128)(2,1)S(1)}, bf16[2,8,4,32,1024]{4,3,2,1,0:T(8,128)(2,1)S(1)}) custom-call(bf16[8,2,32,512]{3,2,1,0:T(8,128)(2,1)S(1)} %reshape.88.rows_in, bf16[4,2,32,1024]{3,2,1,0:T(8,128)(2,1)S(1)} %reshape.89.cols_in), custom_call_target="tpu_custom_call" | custom-call | flops 100000000 | bytes 8000000 | tf_op jit(solution)/shard_map/spread/pallas_call | solution.py:349
  66.3 0.0 copy-start.1
  66.3 1.9 copy-done.1
  68.3 0.0 copy-start
  68.3 0.1 slice.21
  68.4 0.0 copy-done.4
  68.4 3.2 %fusion.15 = f32[1024,1024]{1,0:T(8,128)} fusion(bf16[1024,512]{1,0:T(8,128)(2,1)S(1)} %bitcast.126, bf16[64,8,8,128]{3,2,1,0:T(8,128)(2,1)S(1)} %bitcast.142), kind=kOutput, calls=%fused_computation.14 | convolution fusion | flops 1073741824 | bytes 6291456 | tf_op jit(solution)/shard_map/dot_general | solution.py:431
  71.6 0.0 reduce-scatter.2.cloned.1.call-update
  71.6 2.9 %fusion.1 = f32[64,8,8,128]{3,1,2,0:T(8,128)S(1)} fusion(bf16[2,8,4,32,1024]{4,3,2,1,0:T(8,128)(2,1)} %copy-done.1, bf16[2,8,4,32,512]{4,3,2,1,0:T(8,128)(2,1)S(1)} %get-tuple-element.11), kind=kOutput, calls=%fused_computation.3 | convolution fusion | flops 1074266112 | bytes 5242880 | tf_op jit(solution)/shard_map/dot_general | solution.py:14
  74.5 0.0 copy-start.2
  74.5 1.8 copy.45
  76.3 0.0 copy-done
  76.3 1.1 copy-done.2
  77.4 1.3 fusion.2
  78.7 2.5 %fusion.block = f32[512,1024]{1,0:T(8,128)S(1)} fusion(f32[512,1024,1,1]{1,0,3,2:T(8,128)S(1)} %fusion.2, bf16[2,8,4,32,1024]{4,3,2,1,0:T(8,128)(2,1)S(1)} %copy-done.2, bf16[2,8,4,32,512]{4,3,2,1,0:T(8,128)(2,1)} %copy-done), kind=kOutput, calls=%fused_computation.1 | convolution fusion | flops 1074790400 | bytes 7340032 | tf_op jit(solution)/shard_map/dot_general | solution.py:14
  81.2 0.5 copy.46
  81.7 0.1 slice.28
  81.8 0.1 copy.42
  81.9 111.2 %panel.1 = (f32[16,32,128]{2,1,0:T(8,128)S(1)}, f32[16,32,128]{2,1,0:T(8,128)S(1)}, f32[1,128]{1,0:T(1,128)S(1)}, f32[1,128]{1,0:T(1,128)S(1)}) custom-call(f32[512,1024]{1,0:T(8,128)S(1)} %fusion.block, f32[16,4,128]{2,1,0:T(4,128)S(1)} %select_bitcast_fusion.lead), custom_call_target="tpu_custom_call" | custom-call | flops 400000000 | bytes 4000000 | tf_op jit(solution)/shard_map/panel/pallas_call | solution.py:194
  193.2 0.2 copy.33
  193.3 0.2 copy.31
  193.7 1.9 subtract_bitcast_fusion
  195.6 1.8 copy.51
  197.4 0.5 slice_bitcast_fusion
  197.9 0.0 reduce-scatter.2.cloned.1.call-done
  197.9 1.1 convert_bitcast_fusion
  199.0 0.8 copy.53
  (12 shorter events, 0.3 us)
Async XLA Ops:
  7.2 3.4 %copy-start.3 = (bf16[32,4096]{1,0:T(8,128)(2,1)S(1)}, bf16[32,4096]{1,0:T(8,128)(2,1)}, u32[]{:S(2)}) copy-start(bf16[32,4096]{1,0:T(8,128)(2,1)} %param.3) | copy-start | bytes 786436
  7.2 190.7 %reduce-scatter.2.cloned.1.call-start = ((), (), s32[]{:S(2)}) async-start(), calls=%async_computation.1 | async-start | bytes 4718592 | tf_op jit(solution)/shard_map/reduce_scatter | solution.py:430
  11.7 56.6 %copy-start.4 = (bf16[4,1,128,8,1,128]{5,3,4,2,1,0:T(8,128)(2,1)S(1)}, bf16[4,1,128,8,1,128]{5,3,4,2,1,0:T(8,128)(2,1)}, u32[]{:S(2)}) copy-start(bf16[4,1,128,8,1,128]{5,3,4,2,1,0:T(8,128)(2,1)} %param.5) | copy-start | bytes 3145732
  66.3 1.9 copy-start.1
  68.3 8.0 %copy-start = (bf16[2,8,4,32,512]{4,3,2,1,0:T(8,128)(2,1)}, bf16[2,8,4,32,512]{4,3,2,1,0:T(8,128)(2,1)S(1)}, u32[]{:S(2)}) copy-start(bf16[2,8,4,32,512]{4,3,2,1,0:T(8,128)(2,1)S(1)} %get-tuple-element.11) | copy-start | bytes 6291460
  74.5 2.9 %copy-start.2 = (bf16[2,8,4,32,1024]{4,3,2,1,0:T(8,128)(2,1)S(1)}, bf16[2,8,4,32,1024]{4,3,2,1,0:T(8,128)(2,1)}, u32[]{:S(2)}) copy-start(bf16[2,8,4,32,1024]{4,3,2,1,0:T(8,128)(2,1)} %copy-done.1) | copy-start | bytes 12582916
Sparse Core Ops, SparseCore 0:
  71.7 58.6 reduce-scatter.1
where the time goes:
time: 207 us
  Pallas kernels  166 us (80%)
  between operations  14.3 us (7%)
  local copies, waits for them, and re-layouts  13.2 us (6%)
  matrix products  11.7 us (6%)
    pallas_call x1, Pallas kernels, reduce_panel(): pl.pallas_call(functools.partial(panel_kernel, sizes), out_shape=(jax.Sha...  111 us
    pallas_call x1, Pallas kernels, spread(): pl.pallas_call(functools.partial(spread_kernel, row_count, col_count), ou...  54.6 us
    unnamed x21, local copies, waits for them, and re-layouts  9.07 us
    dot_general x3, matrix products, inner(): lax.dot_general(left, right, (((0,), (0,)), ((), ())), preferred_element_...  6.62 us
  transfers between devices with their start and end apart: 1, of which 0 were waited for; matrix products, arithmetic and copies ran while one was open for 7% of the time, Pallas kernels for 54%

commit v1 on v0

v1 whole, which is shorter than its diff:
```python
import functools

import jax
import jax.numpy as jnp
from jax import lax
from jax.experimental import pallas as pl
from jax.experimental.pallas import tpu as pltpu
from jax.sharding import PartitionSpec as P

PB = 16
LEAD = 32
F32 = jnp.float32
BF16 = jnp.bfloat16
MESH = pl.DeviceIdType.MESH


def inner(left, right):
    return lax.dot_general(
        left, right, (((0,), (0,)), ((), ())), preferred_element_type=F32
    )


def remote(source, target, send, recv, device):
    return pltpu.make_async_remote_copy(
        src_ref=source, dst_ref=target, send_sem=send, recv_sem=recv,
        device_id=device, device_id_type=MESH,
    )


def enter(devices):
    barrier = pltpu.get_barrier_semaphore()
    for device in devices:
        pl.semaphore_signal(barrier, inc=1, device_id=device, device_id_type=MESH)
    pl.semaphore_wait(barrier, len(devices))


def spread_kernel(
    sizes, psi, hpsi, col_all, row_all, lead_all,
    stage, s1_send, s1_recv, up_send, up_recv, down_send, down_recv,
    sib_send, sib_recv, leadz_send, leadz_recv, leadp_send, leadp_recv,
    row_send, row_recv, own_sem,
):
    row_count, col_count, row_tiles, col_tiles, tile = sizes
    levels = row_count // 2
    half = row_tiles * tile
    r = lax.axis_index("row")
    c = lax.axis_index("col")
    z = lax.div(r, 2)
    k = lax.rem(r, 2)
    sib = (r + 1 - 2 * k, c)

    def turn(d):
        return lax.rem(c + d, col_count)

    for target in range(col_count):
        for a, source in enumerate((psi, hpsi)):
            for parity in range(2):
                for t in range(row_tiles):
                    j = target + col_count * parity + row_count * t
                    at = (parity * row_tiles + t) * tile
                    stage[target, a, :, at : at + tile] = source[:, j * tile : (j + 1) * tile]
    col_all[:, z, k, c] = stage[c]

    peers = [(r, turn(d)) for d in range(1, col_count)]
    peers += [(lax.rem(r + 2 * d, row_count), c) for d in range(1, levels)]
    peers += [(sib[0], turn(d)) for d in range(col_count)]
    enter(peers)

    def first(d):
        return remote(
            stage.at[turn(d)], col_all.at[:, z, k, c], s1_send.at[d], s1_recv.at[d], (r, turn(d))
        )

    def first_in(d):
        place = col_all.at[:, z, k, turn(col_count - d)]
        return remote(place, place, s1_send.at[d], s1_recv.at[d], (r, turn(d)))

    def up(o, d):
        place = col_all.at[:, z - o, k, turn(d)]
        return remote(place, place, up_send.at[o, d], up_recv.at[o, d], (r + 2, c))

    def up_in(o, d):
        place = col_all.at[:, z - 1 - o, k, turn(d)]
        return remote(place, place, up_send.at[o, d], up_recv.at[o, d], (r + 2, c))

    def down(o, d):
        place = col_all.at[:, z + o, k, turn(d)]
        return remote(place, place, down_send.at[o, d], down_recv.at[o, d], (r - 2, c))

    def down_in(o, d):
        place = col_all.at[:, z + 1 + o, k, turn(d)]
        return remote(place, place, down_send.at[o, d], down_recv.at[o, d], (r - 2, c))

    def across(level, d):
        place = col_all.at[:, level, k, turn(d)]
        return remote(place, place, sib_send.at[level, d], sib_recv.at[level, d], sib)

    def across_in(level, d):
        place = col_all.at[:, level, 1 - k, turn(d)]
        return remote(place, place, sib_send.at[level, d], sib_recv.at[level, d], sib)

    not_top = z < levels - 1
    not_bottom = z > 0

    def launch(d):
        @pl.when(not_top)
        def _():
            up(0, d).start()

        @pl.when(not_bottom)
        def _():
            down(0, d).start()

        across(z, d).start()

    for d in range(1, col_count):
        first(d).start()
    launch(0)
    order = [col_count - d for d in range(1, col_count)]
    for d in range(1, col_count):
        first_in(d).wait_recv()
        launch(order[d - 1])

    def lead_z(d):
        place = lead_all.at[z, k]
        return remote(
            place, place, leadz_send.at[d], leadz_recv.at[d], (lax.rem(r + 2 * d, row_count), c)
        )

    def lead_z_in(d):
        place = lead_all.at[lax.rem(z + levels - d, levels), k]
        return remote(place, place, leadz_send.at[d], leadz_recv.at[d], (r, c))

    def flat(q):
        return (2 * z + q // col_count, q % col_count)

    def lead_plane(d, q):
        level = lax.rem(z + levels - d, levels)
        place = lead_all.at[level, k]
        return remote(place, place, leadp_send.at[d, q], leadp_recv.at[level, k], flat(q))

    def lead_plane_in(level, kk):
        place = lead_all.at[level, kk]
        return remote(place, place, leadp_send.at[0, 0], leadp_recv.at[level, kk], (r, c))

    def each_peer(action):
        for q in range(2 * col_count):
            @pl.when(k * col_count != q)
            def _():
                action(q)

    @pl.when(c == 0)
    def _():
        for a in range(2):
            block = col_all[a, z, k, :, :, 0:tile].astype(F32)
            block = block.reshape(block.shape[0] * block.shape[1], tile)
            lead_all[z, k, a] = jnp.transpose(block)[0:LEAD].astype(BF16)
        for d in range(1, levels):
            lead_z(d).start()
        each_peer(lambda q: lead_plane(0, q).start())

    source_c = lax.rem(r, col_count)
    source_half = lax.div(r, col_count)
    lane0 = pl.multiple_of(source_half * half, half)
    partner = c + 1 - 2 * lax.rem(c, 2)
    is_source = c == source_c
    is_relay = jnp.logical_and(c != source_c, lax.rem(c, 2) == lax.rem(source_c, 2))

    def row_own(level, kk):
        return pltpu.make_async_copy(
            col_all.at[:, level, kk, :, :, pl.ds(lane0, half)],
            row_all.at[:, level, kk], own_sem.at[level, kk],
        )

    def row_out(level, kk, i):
        device = (r, partner) if i == 0 else (r, lax.rem(c + 2 * i, col_count))
        return remote(
            col_all.at[:, level, kk, :, :, pl.ds(lane0, half)],
            row_all.at[:, level, kk],
            row_send.at[level, kk, i], row_recv.at[level, kk], device,
        )

    def row_relay(level, kk):
        place = row_all.at[:, level, kk]
        return remote(
            place, place, row_send.at[level, kk, 0], row_recv.at[level, kk], (r, partner)
        )

    fan = col_count // 2

    def row_launch(level):
        @pl.when(is_source)
        def _():
            for kk in range(2):
                for i in range(fan):
                    row_out(level, kk, i).start()
                row_own(level, kk).start()

    def row_finish(level):
        @pl.when(is_relay)
        def _():
            for kk in range(2):
                row_relay(level, kk).wait_recv()
                row_relay(level, kk).start()

    def settle(level):
        for d in range(col_count):
            across_in(level, d).wait_recv()
        row_launch(level)

    settle(z)
    for o in range(levels - 1):
        below = z - 1 - o >= 0
        above = z + 1 + o <= levels - 1
        for d in [0] + order:
            @pl.when(below)
            def _():
                up_in(o, d).wait_recv()

                @pl.when(not_top)
                def _():
                    up(o + 1, d).start()

                across(z - 1 - o, d).start()

            @pl.when(above)
            def _():
                down_in(o, d).wait_recv()

                @pl.when(not_bottom)
                def _():
                    down(o + 1, d).start()

                across(z + 1 + o, d).start()

        if o == 0:
            row_finish(z)

            @pl.when(c == 0)
            def _():
                for d in range(1, levels):
                    lead_z_in(d).wait_recv()
                    each_peer(lambda q: lead_plane(d, q).start())
        else:
            @pl.when(z - o >= 0)
            def _():
                row_finish(z - o)

            @pl.when(z + o <= levels - 1)
            def _():
                row_finish(z + o)

        @pl.when(below)
        def _():
            settle(z - 1 - o)

        @pl.when(above)
        def _():
            settle(z + 1 + o)

    @pl.when(z - (levels - 1) >= 0)
    def _():
        row_finish(z - (levels - 1))

    @pl.when(z + levels - 1 <= levels - 1)
    def _():
        row_finish(z + levels - 1)

    for level in range(levels):
        for kk in range(2):
            @pl.when(is_source)
            def _():
                for i in range(fan):
                    row_out(level, kk, i).wait_send()
                row_own(level, kk).wait()

            @pl.when(is_relay)
            def _():
                row_relay(level, kk).wait_send()

            @pl.when(jnp.logical_not(jnp.logical_or(is_source, is_relay)))
            def _():
                row_relay(level, kk).wait_recv()

            @pl.when(jnp.logical_or(c != 0, k != kk))
            def _():
                lead_plane_in(level, kk).wait_recv()

    @pl.when(c == 0)
    def _():
        for d in range(1, levels):
            lead_z(d).wait_send()
        for d in range(levels):
            each_peer(lambda q: lead_plane(d, q).wait_send())

    for d in range(1, col_count):
        first(d).wait_send()
    for o in range(levels):
        for d in range(col_count):
            @pl.when(jnp.logical_and(not_top, z - o >= 0))
            def _():
                up(o, d).wait_send()

            @pl.when(jnp.logical_and(not_bottom, z + o <= levels - 1))
            def _():
                down(o, d).wait_send()

    for level in range(levels):
        for d in range(col_count):
            across(level, d).wait_send()


def spread(psi, hpsi, sizes):
    row_count, col_count, row_tiles, col_tiles, tile = sizes
    g_rows = psi.shape[0]
    levels = row_count // 2
    whole = pl.BlockSpec(memory_space=pltpu.VMEM)
    dma = pltpu.SemaphoreType.DMA
    return pl.pallas_call(
        functools.partial(spread_kernel, sizes),
        out_shape=(
            jax.ShapeDtypeStruct((2, levels, 2, col_count, g_rows, col_tiles * tile), BF16),
            jax.ShapeDtypeStruct((2, levels, 2, col_count, g_rows, row_tiles * tile), BF16),
            jax.ShapeDtypeStruct((levels, 2, 2, LEAD, col_count * g_rows), BF16),
        ),
        in_specs=[whole, whole],
        out_specs=(whole, whole, whole),
        scratch_shapes=[
            pltpu.VMEM((col_count, 2, g_rows, col_tiles * tile), BF16),
            dma((col_count,)), dma((col_count,)),
            dma((levels, col_count)), dma((levels, col_count)),
            dma((levels, col_count)), dma((levels, col_count)),
            dma((levels, col_count)), dma((levels, col_count)),
            dma((levels,)), dma((levels,)),
            dma((levels, 2 * col_count)), dma((levels, 2)),
            dma((levels, 2, col_count // 2)), dma((levels, 2)),
            dma((levels, 2)),
        ],
        compiler_params=pltpu.CompilerParams(
            collective_id=1, has_side_effects=True, vmem_limit_bytes=40 * 1024 * 1024
        ),
        cost_estimate=pl.CostEstimate(
            flops=100_000_000, bytes_accessed=8_000_000, transcendentals=0
        ),
        name="spread",
    )(psi, hpsi)


def lanes_sum(array):
    return jnp.sum(array, axis=1, keepdims=True)


def rows_sum(array):
    return jnp.sum(array, axis=0, keepdims=True)


def parts_of(array):
    high = array.astype(BF16).astype(F32)
    rest = array - high
    middle = rest.astype(BF16).astype(F32)
    return high, middle, rest - middle


def panel_kernel(
    sizes, col_all, lead_all, left, right, diagonal, offdiag,
    natural, turned, panel, vw, message, outgoing, msg_send, msg_recv, end_send, end_recv,
):
    row_count, col_count, row_tiles, col_tiles, tile = sizes
    levels = row_count // 2
    half = row_tiles * tile
    group = 2 * col_count
    r = lax.axis_index("row")
    c = lax.axis_index("col")
    z = lax.div(r, 2)
    k = lax.rem(r, 2)
    part = k * col_count + c
    blocks = levels * 2
    gvecs = natural.shape[1]
    deep = gvecs // blocks

    def peer(d):
        q = lax.rem(part + d, group)
        return (2 * z + lax.div(q, col_count), lax.rem(q, col_count))

    message[...] = jnp.zeros_like(message)
    enter([peer(d) for d in range(1, group)])

    for a in range(2):
        for level in range(levels):
            for kk in range(2):
                at = (level * 2 + kk) * deep
                own = col_all[a, level, kk, :, :, pl.ds(pl.multiple_of(k * half, half), half)]
                own = own.reshape(deep, half)
                natural[a, at : at + deep, 0:half] = own
                turned[a, :, at : at + deep] = jnp.transpose(own.astype(F32)).astype(BF16)
                lead = lead_all[level, kk, a].astype(F32)
                lead = jnp.concatenate(
                    [lead, jnp.zeros((tile - LEAD, deep), F32)], axis=0
                )
                natural[a, at : at + deep, half : half + tile] = jnp.transpose(lead).astype(BF16)
    start = jnp.zeros((LEAD, half + tile), F32)
    for level in range(levels):
        for kk in range(2):
            at = (level * 2 + kk) * deep
            for a in range(2):
                start = start + jnp.dot(
                    lead_all[level, kk, a], natural[1 - a, at : at + deep, :],
                    preferred_element_type=F32,
                )
    panel[...] = 0.5 * start
    vw[...] = jnp.zeros_like(vw)
    diagonal[...] = jnp.zeros_like(diagonal)
    offdiag[...] = jnp.zeros_like(offdiag)

    wide = half + tile
    lane = lax.broadcasted_iota(jnp.int32, (1, wide), 1)
    own_tile = lax.div(lane, tile)
    inside = lane - own_tile * tile
    pos = jnp.where(lane < half, (own_tile * row_count + part) * tile + inside, lane - half)
    lane1 = lax.broadcasted_iota(jnp.int32, (1, tile), 1)
    lane2 = lax.broadcasted_iota(jnp.int32, (2 * PB, tile), 1)
    sub2 = lax.broadcasted_iota(jnp.int32, (2 * PB, tile), 0)
    group_row = lax.broadcasted_iota(jnp.int32, (group, 2 * gvecs + tile), 0)
    sub8 = lax.broadcasted_iota(jnp.int32, (8, half), 0)

    def swap(column):
        return jnp.concatenate([column[PB:], column[:PB]], axis=0)

    def send(slot, d):
        return remote(
            outgoing.at[slot, pl.ds(0, 1)], message.at[slot, pl.ds(part, 1)], msg_send.at[slot, d], msg_recv.at[slot, d], peer(d),
        )

    @pl.loop(0, PB)
    def _(step):
        slot = lax.rem(step, 2)
        both = vw[...]
        lead_vw = both[:, half:]
        head = lanes_sum(jnp.where(lane2 == step, lead_vw, 0.0))
        column = panel[pl.ds(step, 1), :] - rows_sum(both * swap(head))
        below = pos > step + 1
        masked = jnp.where(below, column, 0.0)[:, :half]
        high, middle, low = parts_of(masked)
        stacked = jnp.where(
            sub8 == 0, high, jnp.where(sub8 == 1, middle, jnp.where(sub8 == 2, low, 0.0))
        ).astype(BF16)
        images = []
        for a in range(2):
            image = rows_sum(jnp.dot(stacked, turned[a], preferred_element_type=F32))
            outgoing[slot, 0:1, a * gvecs : (a + 1) * gvecs] = image
            images.append(image)
        onto = lanes_sum(both[:, :half] * masked)
        tail = lanes_sum(masked * masked)
        small = rows_sum(jnp.where(lane2 == sub2, onto, 0.0)) + jnp.where(
            lane1 == 2 * PB, tail, 0.0
        )
        outgoing[slot, 0:1, 2 * gvecs : 2 * gvecs + tile] = small
        mine = jnp.concatenate(images + [small], axis=1)
        sent = [send(slot, d) for d in range(1, group)]
        for copy in sent:
            copy.start()
        lead_column = column[:, half:]
        pivot = lanes_sum(jnp.where(lane1 == step + 1, lead_column, 0.0))
        here = lanes_sum(jnp.where(lane1 == step, lead_column, 0.0))
        next_row = panel[pl.ds(step + 1, 1), :]
        corner = lanes_sum(jnp.where(lane1 == step + 1, next_row[:, half:], 0.0))
        head_next = lanes_sum(jnp.where(lane2 == step + 1, lead_vw, 0.0))
        for copy in sent:
            copy.wait()
        received = message[slot] + jnp.where(group_row == part, mine, 0.0)
        sums = received[:, : 2 * gvecs]
        pieces = jnp.concatenate(parts_of(sums) + (jnp.zeros_like(sums),), axis=0)
        pieces = pieces.astype(BF16)
        product = rows_sum(
            jnp.dot(pieces[:, :gvecs], natural[1], preferred_element_type=F32)
            + jnp.dot(pieces[:, gvecs:], natural[0], preferred_element_type=F32)
        ) * 0.5
        whole_sum = rows_sum(sums)
        square = lanes_sum(whole_sum[:, :gvecs] * whole_sum[:, gvecs:])
        small = rows_sum(received[:, 2 * gvecs :])
        tail = lanes_sum(jnp.where(lane1 == 2 * PB, small, 0.0))
        onto = lanes_sum(jnp.where(lane2 == sub2, small, 0.0))
        length = jnp.sqrt(pivot * pivot + tail)
        beta = jnp.where(pivot >= 0.0, -length, length)
        tau = (beta - pivot) / beta
        inverse = 1.0 / (pivot - beta)
        vector = jnp.where(
            pos == step + 1, 1.0, jnp.where(below, column * inverse, 0.0)
        )
        onto = onto * inverse + head_next
        image = tau * (product * inverse + next_row - rows_sum(both * swap(onto)))
        edge = lanes_sum(jnp.where(lane1 == step + 1, product[:, half:], 0.0))
        energy = square * inverse * inverse + 2.0 * inverse * edge + corner
        overlap = tau * (energy - 2.0 * rows_sum(onto[:PB] * onto[PB:]))
        image = image - 0.5 * tau * overlap * vector
        vw[pl.ds(step, 1), :] = vector
        vw[pl.ds(PB + step, 1), :] = image
        diagonal[...] = jnp.where(lane1 == step, here, diagonal[...])
        offdiag[...] = jnp.where(lane1 == step, beta, offdiag[...])

    final = vw[:, 0:half]
    right[pl.ds(k, 1)] = final[None]
    across = remote(
        right.at[k], right.at[k], end_send.at[col_count], end_recv.at[1], (r + 1 - 2 * k, c)
    )
    across.start()

    def to_row(j):
        return remote(
            right.at[k], left, end_send.at[j], end_recv.at[0], (part, j)
        )

    mine = jnp.logical_and(part >= 2 * z, part < 2 * z + 2)
    for j in range(col_count):
        @pl.when(jnp.logical_and(mine, jnp.logical_not(jnp.logical_and(part == r, c == j))))
        def _():
            to_row(j).start()

    @pl.when(part == r)
    def _():
        left[...] = final

    @pl.when(part != r)
    def _():
        to_row(0).wait_recv()

    across_in = remote(
        right.at[1 - k], right.at[1 - k], end_send.at[col_count], end_recv.at[1], (r, c)
    )
    across_in.wait_recv()
    across.wait_send()
    for j in range(col_count):
        @pl.when(jnp.logical_and(mine, jnp.logical_not(jnp.logical_and(part == r, c == j))))
        def _():
            to_row(j).wait_send()


def reduce_panel(col_all, lead_all, sizes):
    row_count, col_count, row_tiles, col_tiles, tile = sizes
    half = row_tiles * tile
    gvecs = row_count * col_count * col_all.shape[4]
    group = 2 * col_count
    whole = pl.BlockSpec(memory_space=pltpu.VMEM)
    dma = pltpu.SemaphoreType.DMA
    return pl.pallas_call(
        functools.partial(panel_kernel, sizes),
        out_shape=(
            jax.ShapeDtypeStruct((2 * PB, half), F32),
            jax.ShapeDtypeStruct((2, 2 * PB, half), F32),
            jax.ShapeDtypeStruct((1, tile), F32),
            jax.ShapeDtypeStruct((1, tile), F32),
        ),
        in_specs=[whole, whole],
        out_specs=(whole, whole, whole, whole),
        scratch_shapes=[
            pltpu.VMEM((2, gvecs, half + tile), BF16),
            pltpu.VMEM((2, half, gvecs), BF16),
            pltpu.VMEM((LEAD, half + tile), F32),
            pltpu.VMEM((2 * PB, half + tile), F32),
            pltpu.VMEM((2, group, 2 * gvecs + tile), F32),
            pltpu.VMEM((2, 8, 2 * gvecs + tile), F32),
            dma((2, group)), dma((2, group)),
            dma((col_count + 1,)), dma((2,)),
        ],
        compiler_params=pltpu.CompilerParams(
            collective_id=0, has_side_effects=True, vmem_limit_bytes=40 * 1024 * 1024
        ),
        cost_estimate=pl.CostEstimate(
            flops=400_000_000, bytes_accessed=4_000_000, transcendentals=0
        ),
        name="panel",
    )(col_all, lead_all)


def on_device(psi, hpsi, eigvec):
    highest = lax.Precision.HIGHEST
    row_tiles = eigvec.shape[0]
    tile = eigvec.shape[2]
    col_tiles = eigvec.shape[3]
    row_count = lax.axis_size("row")
    col_count = lax.axis_size("col")
    gvecs = psi.shape[0] * row_count * col_count
    row_width = row_tiles * tile
    col_width = col_tiles * tile
    sizes = (row_count, col_count, row_tiles, col_tiles, tile)
    col_all, row_all, lead_all = spread(psi, hpsi, sizes)
    psi_rows = row_all[0].reshape(gvecs, row_width)
    hpsi_rows = row_all[1].reshape(gvecs, row_width)
    psi_cols = col_all[0].reshape(gvecs, col_width)
    hpsi_cols = col_all[1].reshape(gvecs, col_width)
    reduced = 0.5 * (inner(psi_rows, hpsi_cols) + inner(hpsi_rows, psi_cols))
    correlation = inner(psi_rows, psi_cols) / float(gvecs)
    left, right, diagonal, offdiag = reduce_panel(col_all, lead_all, sizes)
    right = jnp.concatenate([right[:, PB:], right[:, :PB]], axis=1)
    right = jnp.concatenate([right[0], right[1]], axis=1)
    updated = reduced - lax.dot_general(
        left, right, (((0,), (0,)), ((), ())), precision=highest,
        preferred_element_type=F32,
    )
    flat = eigvec.reshape(row_width, col_width)
    rotated = lax.psum_scatter(
        jnp.dot(psi_rows, flat, preferred_element_type=F32),
        "row",
        scatter_dimension=0,
        tiled=True,
    )
    tile_shape = (row_tiles, 1, tile, col_tiles, 1, tile)

    def in_order(matrix):
        matrix = matrix.reshape(row_width, 2, row_tiles, tile)
        return jnp.transpose(matrix, (0, 2, 1, 3)).reshape(tile_shape)

    return (
        in_order(correlation),
        in_order(updated),
        diagonal[0, :PB],
        offdiag[0, :PB],
        rotated.astype(BF16).reshape(rotated.shape[0], col_tiles, 1, tile),
    )


def solution(mesh):
    return jax.shard_map(
        on_device,
        mesh=mesh,
        in_specs=(
            P(("row", "col"), None),
            P(("row", "col"), None),
            P(None, "row", None, None, "col", None),
        ),
        out_specs=(
            P(None, "row", None, None, "col", None),
            P(None, "row", None, None, "col", None),
            P(),
            P(),
            P("row", None, "col", None),
        ),
        check_vma=False,
    )
```

time: 207 us -> 183 us (0.88)
  Pallas kernels: 166 us -> 136 us
  local copies, waits for them, and re-layouts: 13.2 us -> 19.3 us
    pallas_call x1, Pallas kernels: 111 us -> 84.1 us  [reduce_panel(): pl.pallas_call(functools.partial(panel_kernel, sizes), out_shape=(jax.Sha...]
    transpose x0 -> x2, local copies, waits for them, and re-layouts: none -> 6.53 us  [in_order(): return jnp.transpose(matrix, (0, 2, 1, 3)).reshape(tile_shape)]
    reshape x4 -> x2, local copies, waits for them, and re-layouts: 0.74 us -> 5.35 us  [in_order(): matrix = matrix.reshape(row_width, 2, row_tiles, tile)]
    pallas_call x1, Pallas kernels: 54.6 us -> 52 us  [spread(): pl.pallas_call(functools.partial(spread_kernel, sizes), out_shape=(jax.Sh...]
    another operation x6 -> x0, local copies, waits for them, and re-layouts: 2.55 us -> none  [spread(): both = jnp.stack([psi, hpsi])]
    unnamed x21 -> x13, local copies, waits for them, and re-layouts: 9.07 us -> 6.78 us
  transfers between devices with their start and end apart: 1 -> 1, of which waited for: 0 -> 0; matrix products, arithmetic and copies ran while one was open for 7% -> 12% of each run, Pallas kernels for 54% -> 46%
where the time goes in v1:
time: 183 us; the launch traced here: 182 us
  Pallas kernels  136 us (74%)
  local copies, waits for them, and re-layouts  19.3 us (11%)
  between operations  14.1 us (8%)
  matrix products  11.8 us (6%)
    pallas_call x1, Pallas kernels, reduce_panel(): pl.pallas_call(functools.partial(panel_kernel, sizes), out_shape=(jax.Sha...  84.1 us
    pallas_call x1, Pallas kernels, spread(): pl.pallas_call(functools.partial(spread_kernel, sizes), out_shape=(jax.Sh...  52 us
    unnamed x13, local copies, waits for them, and re-layouts  6.78 us
    transpose x2, local copies, waits for them, and re-layouts, in_order(): return jnp.transpose(matrix, (0, 2, 1, 3)).reshape(tile_shape)  6.53 us
    reshape x2, local copies, waits for them, and re-layouts, in_order(): matrix = matrix.reshape(row_width, 2, row_tiles, tile)  5.35 us
    dot_general x3, matrix products, inner(): lax.dot_general(left, right, (((0,), (0,)), ((), ())), preferred_element_...  5.13 us
  transfers between devices with their start and end apart: 1, of which 0 were waited for; matrix products, arithmetic and copies ran while one was open for 12% of the time, Pallas kernels for 46%

profile of v1, /device:TPU:0, one launch (start us, length us, event | category | flops | bytes accessed | tf_op | source)
XLA Modules:
  0.0 182.3 jit_solution(18311443479957588756)
XLA Ops:
  7.2 0.0 reduce-scatter.2.cloned.1.call-start
  7.2 0.0 copy-start.3
  7.2 0.9 copy-done.3
  8.2 0.0 copy-start.4
  8.2 0.9 copy-done.4
  9.1 0.0 copy-start.5
  9.1 52.0 %spread.1 = (bf16[2,4,2,4,32,1024]{5,4,3,2,1,0:T(8,128)(2,1)S(1)}, bf16[2,4,2,4,32,512]{5,4,3,2,1,0:T(8,128)(2,1)S(1)}, bf16[4,2,2,32,128]{4,3,2,1,0:T(8,128)(2,1)S(1)}) custom-call(bf16[32,4096]{1,0:T(8,128)(2,1)S(1)} %copy-done.3, bf16[32,4096]{1,0:T(8,128)(2,1)S(1)} %copy-done.4), custom_call_target="tpu_custom_call" | custom-call | flops 100000000 | bytes 8000000 | tf_op jit(solution)/shard_map/spread/pallas_call | solution.py:319
  61.1 0.0 copy-start
  61.1 1.9 %copy-done = bf16[2,4,2,4,32,1024]{5,4,3,2,1,0:T(8,128)(2,1)} copy-done((bf16[2,4,2,4,32,1024]{5,4,3,2,1,0:T(8,128)(2,1)}, bf16[2,4,2,4,32,1024]{5,4,3,2,1,0:T(8,128)(2,1)S(1)}, u32[]{:S(2)}) %copy-start) | copy-done | bytes 4194328
  63.1 0.1 slice.30
  63.1 0.0 copy-done.5
  63.2 3.2 %fusion.13 = f32[1024,1024]{1,0:T(8,128)} fusion(bf16[1024,512]{1,0:T(8,128)(2,1)S(1)} %bitcast.66, bf16[64,8,8,128]{3,2,1,0:T(8,128)(2,1)S(1)} %bitcast.68), kind=kOutput, calls=%fused_computation.13 | convolution fusion | flops 1073741824 | bytes 6291456 | tf_op jit(solution)/shard_map/dot_general | solution.py:602
  66.4 0.0 reduce-scatter.2.cloned.1.call-update
  66.4 0.0 copy-start.1
  66.4 2.2 %copy-done.1 = bf16[2,4,2,4,32,1024]{5,4,3,2,1,0:T(8,128)(2,1)S(1)} copy-done((bf16[2,4,2,4,32,1024]{5,4,3,2,1,0:T(8,128)(2,1)S(1)}, bf16[2,4,2,4,32,1024]{5,4,3,2,1,0:T(8,128)(2,1)}, u32[]{:S(2)}) %copy-start.1) | copy-done | bytes 4194328
  68.6 84.1 %panel.1 = (f32[32,512]{1,0:T(8,128)S(1)}, f32[2,32,512]{2,1,0:T(8,128)S(1)}, f32[1,128]{1,0:T(1,128)S(1)}, f32[1,128]{1,0:T(1,128)S(1)}) custom-call(bf16[2,4,2,4,32,1024]{5,4,3,2,1,0:T(8,128)(2,1)S(1)} %copy-done.1, bf16[4,2,2,32,128]{4,3,2,1,0:T(8,128)(2,1)S(1)} %get-tuple-element.14.lead_all), custom_call_target="tpu_custom_call" | custom-call | flops 400000000 | bytes 4000000 | tf_op jit(solution)/shard_map/panel/pallas_call | solution.py:545
  152.7 1.3 fusion.2
  154.0 1.3 fusion.4
  155.2 3.4 %fusion.1 = f32[512,1024]{1,0:T(8,128)} fusion(f32[512,1024,1,1,1]{1,0,4,3,2:T(8,128)S(1)} %fusion.4, f32[512,1024,1,1,1]{1,0,4,3,2:T(8,128)S(1)} %fusion.2, f32[32,512]{1,0:T(8,128)S(1)} %get-tuple-element.15, f32[32,512]{1,0:T(8,128)S(1)} %get-tuple-element.25, f32[32,512]{1,0:T(8,128)S(1)} %get-tuple-element.24), kind=kOutput, calls=%fused_computation.2 | convolution fusion | flops 202932224 | bytes 6488064 | tf_op jit(solution)/shard_map/dot_general | solution.py:596
  158.6 3.2 %reshape.48 = f32[512,2,4,128]{3,2,1,0:T(4,128)} reshape(f32[512,1024]{1,0:T(8,128)} %fusion.1) | data formatting | bytes 4194304 | tf_op jit(solution)/shard_map/reshape | solution.py:610
  161.8 0.0 copy-start.2
  161.8 4.1 %copy.9 = f32[512,4,2,128]{3,2,1,0:T(2,128)} copy(f32[512,4,2,128]{3,1,2,0:T(4,128)} %bitcast.62) | data formatting | bytes 4194304 | tf_op jit(solution)/shard_map/transpose | solution.py:611
  165.9 0.0 copy-done.2
  165.9 2.6 %bitcast_multiply_fusion = f32[512,1024]{1,0:T(8,128)} fusion(bf16[2,4,2,4,32,1024]{5,4,3,2,1,0:T(8,128)(2,1)S(1)} %copy-done.2, bf16[2,4,2,4,32,512]{5,4,3,2,1,0:T(8,128)(2,1)S(1)} %get-tuple-element.12), kind=kOutput, calls=%fused_computation.3 | convolution fusion | flops 1074266112 | bytes 5242880 | tf_op jit(solution)/shard_map/dot_general | solution.py:18
  168.5 2.2 %reshape.44 = f32[512,2,4,128]{3,2,1,0:T(4,128)S(1)} reshape(f32[512,1024]{1,0:T(8,128)} %bitcast_multiply_fusion) | data formatting | bytes 4194304 | tf_op jit(solution)/shard_map/reshape | solution.py:610
  170.7 2.4 %copy.8 = f32[512,4,2,128]{3,2,1,0:T(2,128)} copy(f32[512,4,2,128]{3,1,2,0:T(4,128)S(1)} %bitcast.63) | data formatting | bytes 4194304 | tf_op jit(solution)/shard_map/transpose | solution.py:611
  173.1 0.5 slice_bitcast_fusion
  173.6 0.0 reduce-scatter.2.cloned.1.call-done
  173.6 1.1 convert_bitcast_fusion
  174.7 0.8 copy.15
  (2 shorter events, 0.0 us)
Async XLA Ops:
  7.2 166.5 %reduce-scatter.2.cloned.1.call-start = ((), (), s32[]{:S(2)}) async-start(), calls=%async_computation.1 | async-start | bytes 4718592 | tf_op jit(solution)/shard_map/reduce_scatter | solution.py:601
  7.2 1.0 copy-start.3
  8.2 0.9 copy-start.4
  9.1 54.0 %copy-start.5 = (bf16[4,1,128,8,1,128]{5,3,4,2,1,0:T(8,128)(2,1)S(1)}, bf16[4,1,128,8,1,128]{5,3,4,2,1,0:T(8,128)(2,1)}, u32[]{:S(2)}) copy-start(bf16[4,1,128,8,1,128]{5,3,4,2,1,0:T(8,128)(2,1)} %param.5) | copy-start | bytes 3145732
  61.1 2.0 %copy-start = (bf16[2,4,2,4,32,1024]{5,4,3,2,1,0:T(8,128)(2,1)}, bf16[2,4,2,4,32,1024]{5,4,3,2,1,0:T(8,128)(2,1)S(1)}, u32[]{:S(2)}) copy-start(bf16[2,4,2,4,32,1024]{5,4,3,2,1,0:T(8,128)(2,1)S(1)} %get-tuple-element.13.col_all) | copy-start | bytes 12582916
  66.4 2.2 %copy-start.1 = (bf16[2,4,2,4,32,1024]{5,4,3,2,1,0:T(8,128)(2,1)S(1)}, bf16[2,4,2,4,32,1024]{5,4,3,2,1,0:T(8,128)(2,1)}, u32[]{:S(2)}) copy-start(bf16[2,4,2,4,32,1024]{5,4,3,2,1,0:T(8,128)(2,1)} %copy-done) | copy-start | bytes 12582916
  161.8 4.1 %copy-start.2 = (bf16[2,4,2,4,32,1024]{5,4,3,2,1,0:T(8,128)(2,1)S(1)}, bf16[2,4,2,4,32,1024]{5,4,3,2,1,0:T(8,128)(2,1)}, u32[]{:S(2)}) copy-start(bf16[2,4,2,4,32,1024]{5,4,3,2,1,0:T(8,128)(2,1)} %copy-done) | copy-start | bytes 12582916
Sparse Core Ops, SparseCore 0:
  66.5 55.8 reduce-scatter.1

commit v2 on v1

--- a/solution.py
+++ b/solution.py
@@ -34,11 +34,30 @@
     pl.semaphore_wait(barrier, len(devices))
 
 
-def spread_kernel(
-    sizes, psi, hpsi, col_all, row_all, lead_all,
-    stage, s1_send, s1_recv, up_send, up_recv, down_send, down_recv,
+def lanes_sum(array):
+    return jnp.sum(array, axis=1, keepdims=True)
+
+
+def rows_sum(array):
+    return jnp.sum(array, axis=0, keepdims=True)
+
+
+def parts_of(array):
+    high = array.astype(BF16).astype(F32)
+    rest = array - high
+    middle = rest.astype(BF16).astype(F32)
+    return high, middle, rest - middle
+
+
+def step_kernel(
+    sizes, psi, hpsi, eig,
+    reduced, correlation, left, right, diagonal, offdiag, rotated,
+    col_all, row_all, lead_all, stage, natural, turned, panel, vw, message, outgoing,
+    keep, give, take, inbox, spun,
+    s1_send, s1_recv, up_send, up_recv, down_send, down_recv,
     sib_send, sib_recv, leadz_send, leadz_recv, leadp_send, leadp_recv,
-    row_send, row_recv, own_sem,
+    row_send, row_recv, own_sem, msg_send, msg_recv, end_send, end_recv,
+    swap_send, swap_recv, sum_send, sum_recv, spin_sem,
 ):
     row_count, col_count, row_tiles, col_tiles, tile = sizes
     levels = row_count // 2
@@ -48,6 +67,17 @@
     z = lax.div(r, 2)
     k = lax.rem(r, 2)
     sib = (r + 1 - 2 * k, c)
+    group = 2 * col_count
+    part = k * col_count + c
+    gvecs = natural.shape[1]
+    deep = gvecs // row_count
+
+    def peer(d):
+        q = lax.rem(part + d, group)
+        return (2 * z + lax.div(q, col_count), lax.rem(q, col_count))
+
+    def along(d):
+        return (lax.rem(r + 2 * d, row_count), c)
 
     def turn(d):
         return lax.rem(c + d, col_count)
@@ -61,10 +91,8 @@
                     stage[target, a, :, at : at + tile] = source[:, j * tile : (j + 1) * tile]
     col_all[:, z, k, c] = stage[c]
 
-    peers = [(r, turn(d)) for d in range(1, col_count)]
-    peers += [(lax.rem(r + 2 * d, row_count), c) for d in range(1, levels)]
-    peers += [(sib[0], turn(d)) for d in range(col_count)]
-    enter(peers)
+    message[...] = jnp.zeros_like(message)
+    enter([peer(d) for d in range(1, group)] + [along(d) for d in range(1, levels)])
 
     def first(d):
         return remote(
@@ -208,6 +236,27 @@
             across_in(level, d).wait_recv()
         row_launch(level)
 
+    def absorb(level):
+        for kk in range(2):
+            at = pl.multiple_of((level * 2 + kk) * deep, deep)
+
+            @pl.when(jnp.logical_or(c != 0, k != kk))
+            def _():
+                lead_plane_in(level, kk).wait_recv()
+
+            for a in range(2):
+                own = col_all[a, level, kk, :, :, pl.ds(pl.multiple_of(k * half, half), half)]
+                own = own.reshape(deep, half)
+                natural[a, pl.ds(at, deep), 0:half] = own
+                turned[a, :, pl.ds(at, deep)] = jnp.transpose(own.astype(F32)).astype(BF16)
+                lead = lead_all[level, kk, a].astype(F32)
+                lead = jnp.concatenate(
+                    [lead, jnp.zeros((tile - LEAD, deep), F32)], axis=0
+                )
+                natural[a, pl.ds(at, deep), half : half + tile] = (
+                    jnp.transpose(lead).astype(BF16)
+                )
+
     settle(z)
     for o in range(levels - 1):
         below = z - 1 - o >= 0
@@ -234,21 +283,24 @@
                 across(z + 1 + o, d).start()
 
         if o == 0:
-            row_finish(z)
-
             @pl.when(c == 0)
             def _():
                 for d in range(1, levels):
                     lead_z_in(d).wait_recv()
                     each_peer(lambda q: lead_plane(d, q).start())
+
+            row_finish(z)
+            absorb(z)
         else:
             @pl.when(z - o >= 0)
             def _():
                 row_finish(z - o)
+                absorb(z - o)
 
             @pl.when(z + o <= levels - 1)
             def _():
                 row_finish(z + o)
+                absorb(z + o)
 
         @pl.when(below)
         def _():
@@ -258,146 +310,17 @@
         def _():
             settle(z + 1 + o)
 
-    @pl.when(z - (levels - 1) >= 0)
+    far_below = z - (levels - 1) >= 0
+    far_above = z + levels - 1 <= levels - 1
+
+    @pl.when(far_below)
     def _():
-        row_finish(z - (levels - 1))
-
-    @pl.when(z + levels - 1 <= levels - 1)
+        absorb(z - (levels - 1))
+
+    @pl.when(far_above)
     def _():
-        row_finish(z + levels - 1)
-
-    for level in range(levels):
-        for kk in range(2):
-            @pl.when(is_source)
-            def _():
-                for i in range(fan):
-                    row_out(level, kk, i).wait_send()
-                row_own(level, kk).wait()
-
-            @pl.when(is_relay)
-            def _():
-                row_relay(level, kk).wait_send()
-
-            @pl.when(jnp.logical_not(jnp.logical_or(is_source, is_relay)))
-            def _():
-                row_relay(level, kk).wait_recv()
-
-            @pl.when(jnp.logical_or(c != 0, k != kk))
-            def _():
-                lead_plane_in(level, kk).wait_recv()
-
-    @pl.when(c == 0)
-    def _():
-        for d in range(1, levels):
-            lead_z(d).wait_send()
-        for d in range(levels):
-            each_peer(lambda q: lead_plane(d, q).wait_send())
-
-    for d in range(1, col_count):
-        first(d).wait_send()
-    for o in range(levels):
-        for d in range(col_count):
-            @pl.when(jnp.logical_and(not_top, z - o >= 0))
-            def _():
-                up(o, d).wait_send()
-
-            @pl.when(jnp.logical_and(not_bottom, z + o <= levels - 1))
-            def _():
-                down(o, d).wait_send()
-
-    for level in range(levels):
-        for d in range(col_count):
-            across(level, d).wait_send()
-
-
-def spread(psi, hpsi, sizes):
-    row_count, col_count, row_tiles, col_tiles, tile = sizes
-    g_rows = psi.shape[0]
-    levels = row_count // 2
-    whole = pl.BlockSpec(memory_space=pltpu.VMEM)
-    dma = pltpu.SemaphoreType.DMA
-    return pl.pallas_call(
-        functools.partial(spread_kernel, sizes),
-        out_shape=(
-            jax.ShapeDtypeStruct((2, levels, 2, col_count, g_rows, col_tiles * tile), BF16),
-            jax.ShapeDtypeStruct((2, levels, 2, col_count, g_rows, row_tiles * tile), BF16),
-            jax.ShapeDtypeStruct((levels, 2, 2, LEAD, col_count * g_rows), BF16),
-        ),
-        in_specs=[whole, whole],
-        out_specs=(whole, whole, whole),
-        scratch_shapes=[
-            pltpu.VMEM((col_count, 2, g_rows, col_tiles * tile), BF16),
-            dma((col_count,)), dma((col_count,)),
-            dma((levels, col_count)), dma((levels, col_count)),
-            dma((levels, col_count)), dma((levels, col_count)),
-            dma((levels, col_count)), dma((levels, col_count)),
-            dma((levels,)), dma((levels,)),
-            dma((levels, 2 * col_count)), dma((levels, 2)),
-            dma((levels, 2, col_count // 2)), dma((levels, 2)),
-            dma((levels, 2)),
-        ],
-        compiler_params=pltpu.CompilerParams(
-            collective_id=1, has_side_effects=True, vmem_limit_bytes=40 * 1024 * 1024
-        ),
-        cost_estimate=pl.CostEstimate(
-            flops=100_000_000, bytes_accessed=8_000_000, transcendentals=0
-        ),
-        name="spread",
-    )(psi, hpsi)
-
-
-def lanes_sum(array):
-    return jnp.sum(array, axis=1, keepdims=True)
-
-
-def rows_sum(array):
-    return jnp.sum(array, axis=0, keepdims=True)
-
-
-def parts_of(array):
-    high = array.astype(BF16).astype(F32)
-    rest = array - high
-    middle = rest.astype(BF16).astype(F32)
-    return high, middle, rest - middle
-
-
-def panel_kernel(
-    sizes, col_all, lead_all, left, right, diagonal, offdiag,
-    natural, turned, panel, vw, message, outgoing, msg_send, msg_recv, end_send, end_recv,
-):
-    row_count, col_count, row_tiles, col_tiles, tile = sizes
-    levels = row_count // 2
-    half = row_tiles * tile
-    group = 2 * col_count
-    r = lax.axis_index("row")
-    c = lax.axis_index("col")
-    z = lax.div(r, 2)
-    k = lax.rem(r, 2)
-    part = k * col_count + c
-    blocks = levels * 2
-    gvecs = natural.shape[1]
-    deep = gvecs // blocks
-
-    def peer(d):
-        q = lax.rem(part + d, group)
-        return (2 * z + lax.div(q, col_count), lax.rem(q, col_count))
-
-    message[...] = jnp.zeros_like(message)
-    enter([peer(d) for d in range(1, group)])
-
-    for a in range(2):
-        for level in range(levels):
-            for kk in range(2):
-                at = (level * 2 + kk) * deep
-                own = col_all[a, level, kk, :, :, pl.ds(pl.multiple_of(k * half, half), half)]
-                own = own.reshape(deep, half)
-                natural[a, at : at + deep, 0:half] = own
-                turned[a, :, at : at + deep] = jnp.transpose(own.astype(F32)).astype(BF16)
-                lead = lead_all[level, kk, a].astype(F32)
-                lead = jnp.concatenate(
-                    [lead, jnp.zeros((tile - LEAD, deep), F32)], axis=0
-                )
-                natural[a, at : at + deep, half : half + tile] = jnp.transpose(lead).astype(BF16)
+        absorb(z + levels - 1)
+
     start = jnp.zeros((LEAD, half + tile), F32)
     for level in range(levels):
         for kk in range(2):
@@ -430,6 +353,114 @@
         return remote(
             outgoing.at[slot, pl.ds(0, 1)], message.at[slot, pl.ds(part, 1)], msg_send.at[slot, d], msg_recv.at[slot, d], peer(d),
         )
+
+
+    def rows_late():
+        @pl.when(far_below)
+        def _():
+            row_finish(z - (levels - 1))
+
+        @pl.when(far_above)
+        def _():
+            row_finish(z + levels - 1)
+
+    def rows_wait():
+        for level in range(levels):
+            for kk in range(2):
+                @pl.when(is_source)
+                def _():
+                    row_own(level, kk).wait()
+
+                @pl.when(jnp.logical_not(jnp.logical_or(is_source, is_relay)))
+                def _():
+                    row_relay(level, kk).wait_recv()
+
+    chunk_lanes = half
+
+    def block_work(index):
+        at = pl.multiple_of(lax.div(index, 2) * tile, tile)
+        to = pl.multiple_of(lax.rem(index, 2) * half, half)
+
+        def rows_of(a):
+            return row_all[a, :, :, :, :, pl.ds(at, tile)].reshape(gvecs, tile)
+
+        def cols_of(a):
+            return col_all[a, :, :, :, :, pl.ds(to, half)].reshape(gvecs, half)
+
+        correlation[pl.ds(at, tile), pl.ds(to, half)] = inner(rows_of(0), cols_of(0)) * (
+            1.0 / gvecs
+        )
+        reduced[pl.ds(at, tile), pl.ds(to, half)] = 0.5 * (
+            inner(rows_of(0), cols_of(1)) + inner(rows_of(1), cols_of(0))
+        )
+
+    def swap_copy(level):
+        return remote(
+            give.at[level], take.at[level], swap_send.at[level], swap_recv.at[level], sib
+        )
+
+    def sum_copy(d):
+        level = lax.rem(z + d, levels)
+        return remote(
+            keep.at[level], inbox.at[d], sum_send.at[d], sum_recv.at[d], along(d)
+        )
+
+    def rotate(index):
+        level = lax.rem(z + 1 + index, levels)
+        for kk, target in ((k, keep), (1 - k, give)):
+            rows = row_all[0, level, kk].reshape(deep, half)
+            target[level] = jnp.dot(rows, eig[...], preferred_element_type=F32)
+        swap_copy(level).start()
+
+    def combine(d):
+        level = lax.rem(z + d, levels)
+        swap_copy(level).wait_recv()
+        keep[level] = keep[level] + take[level]
+        if d < levels:
+            sum_copy(d).start()
+
+    def gather_sums():
+        result = keep[z]
+        for d in range(1, levels):
+            sum_copy(d).wait_recv()
+            result = result + inbox[d]
+        inbox[0] = result
+        moves = []
+        for g in range(col_tiles):
+            moves.append(pltpu.make_async_copy(
+                inbox.at[0, :, g * tile : (g + 1) * tile], spun.at[:, g], spin_sem.at[g]
+            ))
+        for move in moves:
+            move.start()
+        for move in moves:
+            move.wait()
+        rotated[...] = spun[...].astype(BF16)
+
+    def background(step):
+        @pl.when(step == 0)
+        def _():
+            rows_late()
+
+        @pl.when(step == 2)
+        def _():
+            rows_wait()
+
+        @pl.when(jnp.logical_and(step > 2, step < 3 + levels))
+        def _():
+            rotate(step - 3)
+
+        for d in range(1, levels + 1):
+            @pl.when(step == 3 + d)
+            def _():
+                combine(d)
+
+        @pl.when(jnp.logical_and(step > 4, step < 5 + 2 * row_tiles))
+        def _():
+            block_work(step - 5)
+
+        @pl.when(step == PB - 2)
+        def _():
+            gather_sums()
 
     @pl.loop(0, PB)
     def _(step):
@@ -459,6 +490,7 @@
         sent = [send(slot, d) for d in range(1, group)]
         for copy in sent:
             copy.start()
+        background(step)
         lead_column = column[:, half:]
         pivot = lanes_sum(jnp.where(lane1 == step + 1, lead_column, 0.0))
         here = lanes_sum(jnp.where(lane1 == step, lead_column, 0.0))
@@ -500,10 +532,10 @@
 
     final = vw[:, 0:half]
     right[pl.ds(k, 1)] = final[None]
-    across = remote(
+    trade = remote(
         right.at[k], right.at[k], end_send.at[col_count], end_recv.at[1], (r + 1 - 2 * k, c)
     )
-    across.start()
+    trade.start()
 
     def to_row(j):
         return remote(
@@ -524,98 +556,192 @@
     def _():
         to_row(0).wait_recv()
 
-    across_in = remote(
+    trade_in = remote(
         right.at[1 - k], right.at[1 - k], end_send.at[col_count], end_recv.at[1], (r, c)
     )
-    across_in.wait_recv()
-    across.wait_send()
+    trade_in.wait_recv()
+    trade.wait_send()
     for j in range(col_count):
         @pl.when(jnp.logical_and(mine, jnp.logical_not(jnp.logical_and(part == r, c == j))))
         def _():
             to_row(j).wait_send()
 
-
-def reduce_panel(col_all, lead_all, sizes):
+    for level in range(levels):
+        swap_copy(level).wait_send()
+    for d in range(1, levels):
+        sum_copy(d).wait_send()
+
+    for level in range(levels):
+        for kk in range(2):
+            @pl.when(is_source)
+            def _():
+                for i in range(fan):
+                    row_out(level, kk, i).wait_send()
+
+            @pl.when(is_relay)
+            def _():
+                row_relay(level, kk).wait_send()
+
+    @pl.when(c == 0)
+    def _():
+        for d in range(1, levels):
+            lead_z(d).wait_send()
+        for d in range(levels):
+            each_peer(lambda q: lead_plane(d, q).wait_send())
+
+    for d in range(1, col_count):
+        first(d).wait_send()
+    for o in range(levels):
+        for d in range(col_count):
+            @pl.when(jnp.logical_and(not_top, z - o >= 0))
+            def _():
+                up(o, d).wait_send()
+
+            @pl.when(jnp.logical_and(not_bottom, z + o <= levels - 1))
+            def _():
+                down(o, d).wait_send()
+
+    for level in range(levels):
+        for d in range(col_count):
+            across(level, d).wait_send()
+
+
+def step(psi, hpsi, eig, sizes):
     row_count, col_count, row_tiles, col_tiles, tile = sizes
+    g_rows = psi.shape[0]
     half = row_tiles * tile
-    gvecs = row_count * col_count * col_all.shape[4]
+    levels = row_count // 2
+    gvecs = row_count * col_count * g_rows
+    deep = gvecs // row_count
     group = 2 * col_count
     whole = pl.BlockSpec(memory_space=pltpu.VMEM)
     dma = pltpu.SemaphoreType.DMA
     return pl.pallas_call(
-        functools.partial(panel_kernel, sizes),
+        functools.partial(step_kernel, sizes),
         out_shape=(
+            jax.ShapeDtypeStruct((half, col_tiles * tile), F32),
+            jax.ShapeDtypeStruct((half, col_tiles * tile), F32),
             jax.ShapeDtypeStruct((2 * PB, half), F32),
             jax.ShapeDtypeStruct((2, 2 * PB, half), F32),
             jax.ShapeDtypeStruct((1, tile), F32),
             jax.ShapeDtypeStruct((1, tile), F32),
+            jax.ShapeDtypeStruct((deep, col_tiles, tile), BF16),
         ),
-        in_specs=[whole, whole],
-        out_specs=(whole, whole, whole, whole),
+        in_specs=[whole] * 3,
+        out_specs=(whole,) * 7,
         scratch_shapes=[
+            pltpu.VMEM((2, levels, 2, col_count, g_rows, col_tiles * tile), BF16),
+            pltpu.VMEM((2, levels, 2, col_count, g_rows, half), BF16),
+            pltpu.VMEM((levels, 2, 2, LEAD, deep), BF16),
+            pltpu.VMEM((col_count, 2, g_rows, col_tiles * tile), BF16),
             pltpu.VMEM((2, gvecs, half + tile), BF16),
             pltpu.VMEM((2, half, gvecs), BF16),
             pltpu.VMEM((LEAD, half + tile), F32),
             pltpu.VMEM((2 * PB, half + tile), F32),
             pltpu.VMEM((2, group, 2 * gvecs + tile), F32),
             pltpu.VMEM((2, 8, 2 * gvecs + tile), F32),
+            pltpu.VMEM((levels, deep, col_tiles * tile), F32),
+            pltpu.VMEM((levels, deep, col_tiles * tile), F32),
+            pltpu.VMEM((levels, deep, col_tiles * tile), F32),
+            pltpu.VMEM((levels, deep, col_tiles * tile), F32),
+            pltpu.VMEM((deep, col_tiles, tile), F32),
+            dma((col_count,)), dma((col_count,)),
+            dma((levels, col_count)), dma((levels, col_count)),
+            dma((levels, col_count)), dma((levels, col_count)),
+            dma((levels, col_count)), dma((levels, col_count)),
+            dma((levels,)), dma((levels,)),
+            dma((levels, group)), dma((levels, 2)),
+            dma((levels, 2, col_count // 2)), dma((levels, 2)),
+            dma((levels, 2)),
             dma((2, group)), dma((2, group)),
             dma((col_count + 1,)), dma((2,)),
+            dma((levels,)), dma((levels,)),
+            dma((levels,)), dma((levels,)),
+            dma((col_tiles,)),
         ],
         compiler_params=pltpu.CompilerParams(
-            collective_id=0, has_side_effects=True, vmem_limit_bytes=40 * 1024 * 1024
+            collective_id=0, has_side_effects=True, vmem_limit_bytes=56 * 1024 * 1024
         ),
         cost_estimate=pl.CostEstimate(
             flops=400_000_000, bytes_accessed=4_000_000, transcendentals=0
         ),
-        name="panel",
-    )(col_all, lead_all)
+        name="step",
+    )(psi, hpsi, eig)
+
+
+def finish_kernel(sizes, reduced, correlation, left, right, updated_out, corr_out, updated, sems):
+    row_count, col_count, row_tiles, col_tiles, tile = sizes
+
+    def place(position):
+        return 2 * (position % row_tiles) + position // row_tiles
+
+    moves = []
+    for position in range(col_tiles):
+        move = pltpu.make_async_copy(
+            correlation.at[:, position * tile : (position + 1) * tile],
+            corr_out.at[:, place(position)], sems.at[position],
+        )
+        move.start()
+        moves.append(move)
+    high, middle, low = parts_of(left[...])
+    lhs = jnp.concatenate([high, high, middle, middle, high, low], axis=0).astype(BF16)
+    for parity in range(2):
+        other = right[parity]
+        other = jnp.concatenate([other[PB:], other[:PB]], axis=0)
+        high, middle, low = parts_of(other)
+        rhs = jnp.concatenate([high, middle, high, middle, low, high], axis=0).astype(BF16)
+        width = row_tiles * tile
+        at = parity * width
+        updated[:, at : at + width] = reduced[:, at : at + width] - inner(lhs, rhs)
+        for t in range(row_tiles):
+            position = parity * row_tiles + t
+            move = pltpu.make_async_copy(
+                updated.at[:, position * tile : (position + 1) * tile],
+                updated_out.at[:, place(position)], sems.at[col_tiles + position],
+            )
+            move.start()
+            moves.append(move)
+    for move in moves:
+        move.wait()
+
+
+def finish(reduced, correlation, left, right, sizes):
+    row_count, col_count, row_tiles, col_tiles, tile = sizes
+    whole = pl.BlockSpec(memory_space=pltpu.VMEM)
+    shape = (row_tiles * tile, col_tiles, tile)
+    return pl.pallas_call(
+        functools.partial(finish_kernel, sizes),
+        out_shape=(jax.ShapeDtypeStruct(shape, F32), jax.ShapeDtypeStruct(shape, F32)),
+        in_specs=[whole] * 4,
+        out_specs=(pl.BlockSpec(memory_space=pl.ANY),) * 2,
+        scratch_shapes=[
+            pltpu.VMEM((row_tiles * tile, col_tiles * tile), F32),
+            pltpu.SemaphoreType.DMA((2 * col_tiles,)),
+        ],
+        cost_estimate=pl.CostEstimate(
+            flops=200_000_000, bytes_accessed=8_000_000, transcendentals=0
+        ),
+        name="finish",
+    )(reduced, correlation, left, right)
 
 
 def on_device(psi, hpsi, eigvec):
-    highest = lax.Precision.HIGHEST
     row_tiles = eigvec.shape[0]
     tile = eigvec.shape[2]
     col_tiles = eigvec.shape[3]
     row_count = lax.axis_size("row")
     col_count = lax.axis_size("col")
-    gvecs = psi.shape[0] * row_count * col_count
-    row_width = row_tiles * tile
-    col_width = col_tiles * tile
     sizes = (row_count, col_count, row_tiles, col_tiles, tile)
-    col_all, row_all, lead_all = spread(psi, hpsi, sizes)
-    psi_rows = row_all[0].reshape(gvecs, row_width)
-    hpsi_rows = row_all[1].reshape(gvecs, row_width)
-    psi_cols = col_all[0].reshape(gvecs, col_width)
-    hpsi_cols = col_all[1].reshape(gvecs, col_width)
-    reduced = 0.5 * (inner(psi_rows, hpsi_cols) + inner(hpsi_rows, psi_cols))
-    correlation = inner(psi_rows, psi_cols) / float(gvecs)
-    left, right, diagonal, offdiag = reduce_panel(col_all, lead_all, sizes)
-    right = jnp.concatenate([right[:, PB:], right[:, :PB]], axis=1)
-    right = jnp.concatenate([right[0], right[1]], axis=1)
-    updated = reduced - lax.dot_general(
-        left, right, (((0,), (0,)), ((), ())), precision=highest,
-        preferred_element_type=F32,
-    )
-    flat = eigvec.reshape(row_width, col_width)
-    rotated = lax.psum_scatter(
-        jnp.dot(psi_rows, flat, preferred_element_type=F32),
-        "row",
-        scatter_dimension=0,
-        tiled=True,
-    )
+    flat = eigvec.reshape(row_tiles * tile, col_tiles * tile)
+    reduced, correlation, left, right, diagonal, offdiag, rotated = step(psi, hpsi, flat, sizes)
+    updated, correlation = finish(reduced, correlation, left, right, sizes)
     tile_shape = (row_tiles, 1, tile, col_tiles, 1, tile)
-
-    def in_order(matrix):
-        matrix = matrix.reshape(row_width, 2, row_tiles, tile)
-        return jnp.transpose(matrix, (0, 2, 1, 3)).reshape(tile_shape)
-
     return (
-        in_order(correlation),
-        in_order(updated),
+        correlation.reshape(tile_shape),
+        updated.reshape(tile_shape),
         diagonal[0, :PB],
         offdiag[0, :PB],
-        rotated.astype(BF16).reshape(rotated.shape[0], col_tiles, 1, tile),
+        rotated.reshape(rotated.shape[0], col_tiles, 1, tile),
     )
 
 

time: 183 us -> 140 us (0.77)
  local copies, waits for them, and re-layouts: 19.3 us -> 3.71 us
  between operations: 14.1 us -> 0.69 us
  matrix products: 11.8 us -> 0 us
    dot_general x5 -> x0, matrix products: 11.8 us -> none  [the longest x3 5.13 us: inner(): lax.dot_general(left, right, (((0,), (0,)), ((), ())), preferred_element_...]
    transpose x2 -> x0, local copies, waits for them, and re-layouts: 6.53 us -> none  [in_order(): return jnp.transpose(matrix, (0, 2, 1, 3)).reshape(tile_shape)]
    reshape x2 -> x0, local copies, waits for them, and re-layouts: 5.35 us -> none  [in_order(): matrix = matrix.reshape(row_width, 2, row_tiles, tile)]
    unnamed x13 -> x8, local copies, waits for them, and re-layouts: 6.78 us -> 3.19 us
  transfers between devices with their start and end apart: 1 -> 0, of which waited for: 0 -> 0; matrix products, arithmetic and copies ran while one was open for 12% -> 0% of each run, Pallas kernels for 46% -> 0%
where the time goes in v2:
time: 140 us; the launch traced here: 139 us
  Pallas kernels  135 us (96%)
  local copies, waits for them, and re-layouts  3.71 us (3%)
    pallas_call x1, Pallas kernels, step(): pl.pallas_call(functools.partial(step_kernel, sizes), out_shape=(jax.Shap...  130 us
    pallas_call x1, Pallas kernels, finish(): pl.pallas_call(functools.partial(finish_kernel, sizes), out_shape=(jax.Sh...  4.4 us
    unnamed x8, local copies, waits for them, and re-layouts  3.19 us

profile of v2, /device:TPU:0, one launch (start us, length us, event | category | flops | bytes accessed | tf_op | source)
XLA Modules:
  0.0 139.2 jit_solution(15193487585044147954)
XLA Ops:
  0.6 2.5 %copy.13 = bf16[64,8,8,128]{3,1,2,0:T(8,128)(2,1)} copy(bf16[64,8,8,128]{3,2,1,0:T(8,128)(2,1)} %bitcast.20) | data formatting | bytes 2097152
  3.1 130.4 %step.1 = (f32[512,1024]{1,0:T(8,128)}, f32[512,1024]{1,0:T(8,128)}, f32[32,512]{1,0:T(8,128)}, f32[2,32,512]{2,1,0:T(8,128)}, f32[1,128]{1,0:T(1,128)}, /*index=5*/f32[1,128]{1,0:T(1,128)}, bf16[128,8,128]{2,1,0:T(8,128)(2,1)}) custom-call(bf16[32,4096]{1,0:T(8,128)(2,1)} %psi.1, bf16[32,4096]{1,0:T(8,128)(2,1)} %hpsi.1, bf16[512,1024]{1,0:T(8,128)(2,1)} %bitcast.19), custom_call_target="tpu_custom_call" | custom-call | flops 400000000 | bytes 4000000 | tf_op jit(solution)/shard_map/step/pallas_call | solution.py:619
  133.5 0.0 copy-start.1
  133.6 0.0 copy-start.2
  133.6 0.0 copy-start
  133.6 4.4 %finish.1 = (f32[512,8,128]{2,1,0:T(8,128)}, f32[512,8,128]{2,1,0:T(8,128)}) custom-call(f32[512,1024]{1,0:T(8,128)} %get-tuple-element.14.reduced, f32[512,1024]{1,0:T(8,128)} %get-tuple-element.15.correlation, f32[32,512]{1,0:T(8,128)} %get-tuple-element.16.left, f32[2,32,512]{2,1,0:T(8,128)} %get-tuple-element.17.right), custom_call_target="tpu_custom_call" | custom-call | flops 200000000 | bytes 8000000 | tf_op jit(solution)/shard_map/finish/pallas_call | solution.py:712
  138.0 0.0 copy-done.1
  138.0 0.0 copy-done.2
  138.0 0.5 slice_bitcast_fusion
  138.5 0.0 copy-done
  138.5 0.7 copy.15
Async XLA Ops:
  133.5 4.4 %copy-start.1 = (f32[1,128]{1,0:T(1,128)S(1)}, f32[1,128]{1,0:T(1,128)}, u32[]{:S(2)}) copy-start(f32[1,128]{1,0:T(1,128)} %get-tuple-element.20) | copy-start | bytes 1540
  133.6 4.4 %copy-start.2 = (f32[1,128]{1,0:T(1,128)S(1)}, f32[1,128]{1,0:T(1,128)}, u32[]{:S(2)}) copy-start(f32[1,128]{1,0:T(1,128)} %get-tuple-element.21) | copy-start | bytes 1540
  133.6 5.0 %copy-start = (bf16[128,8,128]{2,1,0:T(8,128)(2,1)S(1)}, bf16[128,8,128]{2,1,0:T(8,128)(2,1)}, u32[]{:S(2)}) copy-start(bf16[128,8,128]{2,1,0:T(8,128)(2,1)} %get-tuple-element.22) | copy-start | bytes 786436

commit v3 on v2

v3 whole, which is shorter than its diff:
```python
import functools

import jax
import jax.numpy as jnp
from jax import lax
from jax.experimental import pallas as pl
from jax.experimental.pallas import tpu as pltpu
from jax.sharding import PartitionSpec as P

PB = 16
LEAD = 32
F32 = jnp.float32
BF16 = jnp.bfloat16
MESH = pl.DeviceIdType.MESH


def inner(left, right):
    return lax.dot_general(
        left, right, (((0,), (0,)), ((), ())), preferred_element_type=F32
    )


def remote(source, target, send, recv, device):
    return pltpu.make_async_remote_copy(
        src_ref=source, dst_ref=target, send_sem=send, recv_sem=recv,
        device_id=device, device_id_type=MESH,
    )


def enter(devices):
    barrier = pltpu.get_barrier_semaphore()
    for device in devices:
        pl.semaphore_signal(barrier, inc=1, device_id=device, device_id_type=MESH)
    pl.semaphore_wait(barrier, len(devices))


def lanes_sum(array):
    return jnp.sum(array, axis=1, keepdims=True)


def rows_sum(array):
    return jnp.sum(array, axis=0, keepdims=True)


def parts_of(array):
    high = array.astype(BF16).astype(F32)
    rest = array - high
    middle = rest.astype(BF16).astype(F32)
    return high, middle, rest - middle


EARLY = 5


def step_kernel(
    sizes, psi, hpsi, eig,
    reduced, ordered, left, right, ends, rotated,
    correlation, col_all, row_all, lead_all, stage, natural, turned, panel, partial, vw,
    message, outgoing, zmessage, zoutgoing, eig_other, keep, inbox, spun, spun_other,
    s1_send, s1_recv, up_send, up_recv, down_send, down_recv, sib_send, sib_recv,
    leadz_send, leadz_recv, leadp_send, leadp_recv, row_send, row_recv, own_sem,
    give_send, give_recv, msg_send, msg_recv, zmsg_send, zmsg_recv,
    end_send, end_recv, eig_send, eig_recv, sum_send, sum_recv, spin_sem, order_sem,
    spin_send, spin_recv,
):
    row_count, col_count, row_tiles, col_tiles, tile = sizes
    levels = row_count // 2
    half = row_tiles * tile
    full = 2 * half
    wide = full + tile
    gvecs = natural.shape[1]
    deep = gvecs // row_count
    pair = 2 * deep
    r = lax.axis_index("row")
    c = lax.axis_index("col")
    z = lax.div(r, 2)
    k = lax.rem(r, 2)
    is_main = k == 1
    sib = (r + 1 - 2 * k, c)
    partner = c + 1 - 2 * lax.rem(c, 2)
    group = 2 * col_count
    flat_id = k * col_count + c

    def peer(d):
        q = lax.rem(flat_id + d, group)
        return (2 * z + lax.div(q, col_count), lax.rem(q, col_count))

    def along(d):
        return (lax.rem(r + 2 * d, row_count), c)

    def turn(d):
        return lax.rem((partner if d % 2 else c) + 2 * (d // 2), col_count)

    def back(d):
        return d if d < 2 else col_count - d + 2 * (d % 2)

    order = [0] + [back(d) for d in range(1, col_count)]

    for target in range(col_count):
        for a, source in enumerate((psi, hpsi)):
            for parity in range(2):
                for t in range(row_tiles):
                    j = target + col_count * parity + row_count * t
                    at = (parity * row_tiles + t) * tile
                    stage[target, a, :, at : at + tile] = source[:, j * tile : (j + 1) * tile]
    col_all[:, z, k, c] = stage[c]
    message[...] = jnp.zeros_like(message)
    zmessage[...] = jnp.zeros_like(zmessage)
    enter([peer(d) for d in range(1, group)] + [along(d) for d in range(1, levels)])

    def first(d):
        return remote(
            stage.at[turn(d)], col_all.at[:, z, k, c], s1_send.at[d], s1_recv.at[d], (r, turn(d))
        )

    def first_in(d):
        place = col_all.at[:, z, k, turn(back(d))]
        return remote(place, place, s1_send.at[d], s1_recv.at[d], (r, turn(d)))

    def across(level, kk, d):
        place = col_all.at[:, level, kk, turn(d)]
        return remote(
            place, place, sib_send.at[level, kk, d], sib_recv.at[level, kk, d], sib
        )

    def eig_copy():
        return remote(eig, eig_other, eig_send.at[0], eig_recv.at[0], sib)

    def row_give(level, kk):
        place = row_all.at[1, :, level, kk]
        return remote(place, place, give_send.at[level, kk], give_recv.at[level, kk], sib)

    def spin_give():
        return remote(spun_other, rotated, spin_send.at[0], spin_recv.at[0], sib)

    def source_c(kc):
        return lax.rem(2 * z + kc, col_count)

    def source_half(kc):
        return lax.div(2 * z + kc, col_count)

    def block_work(index, kc):
        at = pl.multiple_of(lax.div(index, 2) * tile, tile)
        to = pl.multiple_of(lax.rem(index, 2) * half, half)

        def rows_of(a):
            return row_all[kc, a, :, :, :, :, pl.ds(at, tile)].reshape(gvecs, tile)

        def cols_of(a):
            return col_all[a, :, :, :, :, pl.ds(to, half)].reshape(gvecs, half)

        correlation[pl.ds(at, tile), pl.ds(to, half)] = inner(rows_of(0), cols_of(0)) * (
            1.0 / gvecs
        )
        reduced[pl.ds(at, tile), pl.ds(to, half)] = 0.5 * (
            inner(rows_of(0), cols_of(1)) + inner(rows_of(1), cols_of(0))
        )

    def order_copy(position):
        return pltpu.make_async_copy(
            correlation.at[:, position * tile : (position + 1) * tile],
            ordered.at[:, 2 * (position % row_tiles) + position // row_tiles],
            order_sem.at[position],
        )

    def order_start():
        for position in range(col_tiles):
            order_copy(position).start()

    def order_wait():
        for position in range(col_tiles):
            order_copy(position).wait()

    def helper_core():
        not_top = z < levels - 1
        not_bottom = z > 0

        def up(o, kk, d):
            place = col_all.at[:, z - o, kk, turn(d)]
            return remote(place, place, up_send.at[o, kk, d], up_recv.at[o, kk, d], (r + 2, c))

        def up_in(o, kk, d):
            place = col_all.at[:, z - 1 - o, kk, turn(d)]
            return remote(place, place, up_send.at[o, kk, d], up_recv.at[o, kk, d], (r + 2, c))

        def down(o, kk, d):
            place = col_all.at[:, z + o, kk, turn(d)]
            return remote(
                place, place, down_send.at[o, kk, d], down_recv.at[o, kk, d], (r - 2, c)
            )

        def down_in(o, kk, d):
            place = col_all.at[:, z + 1 + o, kk, turn(d)]
            return remote(
                place, place, down_send.at[o, kk, d], down_recv.at[o, kk, d], (r - 2, c)
            )

        def launch(kk, d):
            @pl.when(not_top)
            def _():
                up(0, kk, d).start()

            @pl.when(not_bottom)
            def _():
                down(0, kk, d).start()

        fan = col_count // 2

        def is_source(kc):
            return c == source_c(kc)

        def is_relay(kc):
            return jnp.logical_and(
                c != source_c(kc), lax.rem(c, 2) == lax.rem(source_c(kc), 2)
            )

        def row_from(kc, level, kk):
            lane0 = pl.multiple_of(source_half(kc) * half, half)
            return col_all.at[:, level, kk, :, :, pl.ds(lane0, half)]

        def row_own(kc, level, kk):
            return pltpu.make_async_copy(
                row_from(kc, level, kk), row_all.at[kc, :, level, kk], own_sem.at[kc, level, kk]
            )

        def row_out(kc, level, kk, i):
            device = (r, partner) if i == 0 else (r, lax.rem(c + 2 * i, col_count))
            return remote(
                row_from(kc, level, kk), row_all.at[kc, :, level, kk],
                row_send.at[kc, level, kk, i], row_recv.at[kc, level, kk], device,
            )

        def row_relay(kc, level, kk):
            place = row_all.at[kc, :, level, kk]
            return remote(
                place, place, row_send.at[kc, level, kk, 0], row_recv.at[kc, level, kk],
                (r, partner),
            )

        def row_launch(level):
            for kc in range(2):
                @pl.when(is_source(kc))
                def _():
                    for kk in range(2):
                        for i in range(fan):
                            row_out(kc, level, kk, i).start()
                        row_own(kc, level, kk).start()

        def row_finish(level):
            for kc in range(2):
                @pl.when(is_relay(kc))
                def _():
                    for kk in range(2):
                        row_relay(kc, level, kk).wait_recv()
                        row_relay(kc, level, kk).start()

        for d in order:
            if d != 0:
                first_in(back(d)).wait_recv()
            launch(0, d)
            across(z, 0, d).start()
            across(z, 1, d).wait_recv()
            launch(1, d)
        row_launch(z)
        for o in range(levels - 1):
            below = z - 1 - o >= 0
            above = z + 1 + o <= levels - 1
            for d in order:
                for kk in range(2):
                    @pl.when(below)
                    def _():
                        up_in(o, kk, d).wait_recv()

                        @pl.when(not_top)
                        def _():
                            up(o + 1, kk, d).start()

                        across(z - 1 - o, kk, d).start()

                    @pl.when(above)
                    def _():
                        down_in(o, kk, d).wait_recv()

                        @pl.when(not_bottom)
                        def _():
                            down(o + 1, kk, d).start()

                        across(z + 1 + o, kk, d).start()

            @pl.when(below)
            def _():
                row_launch(z - 1 - o)

            @pl.when(above)
            def _():
                row_launch(z + 1 + o)

            if o == 0:
                row_finish(z)
            else:
                @pl.when(z - o >= 0)
                def _():
                    row_finish(z - o)

                @pl.when(z + o <= levels - 1)
                def _():
                    row_finish(z + o)

        @pl.when(z - (levels - 1) >= 0)
        def _():
            row_finish(z - (levels - 1))

        @pl.when(z + levels - 1 <= levels - 1)
        def _():
            row_finish(z + levels - 1)

        for level in range(levels):
            for kk in range(2):
                for kc in range(2):
                    @pl.when(is_source(kc))
                    def _():
                        row_own(kc, level, kk).wait()

                    @pl.when(jnp.logical_not(jnp.logical_or(is_source(kc), is_relay(kc))))
                    def _():
                        row_relay(kc, level, kk).wait_recv()

                row_give(level, kk).start()
        eig_copy().wait_recv()

        def sum_copy(d):
            return remote(
                keep.at[lax.rem(z + d, levels)], inbox.at[d], sum_send.at[d], sum_recv.at[d],
                along(d),
            )

        for i in range(levels):
            level = lax.rem(z + 1 + i, levels)
            keep[level] = jnp.dot(
                row_all[0, 0, level].reshape(pair, half), eig[...], preferred_element_type=F32
            ) + jnp.dot(
                row_all[1, 0, level].reshape(pair, half), eig_other[...],
                preferred_element_type=F32,
            )
            if i < levels - 1:
                sum_copy(i + 1).start()

        @pl.loop(0, 2 * row_tiles)
        def _(index):
            block_work(index, 0)

        order_start()
        result = keep[z]
        for d in range(1, levels):
            sum_copy(d).wait_recv()
            result = result + inbox[d]
        inbox[0] = result
        moves = []
        for kk in range(2):
            for g in range(col_tiles):
                moves.append(pltpu.make_async_copy(
                    inbox.at[0, kk * deep : (kk + 1) * deep, g * tile : (g + 1) * tile],
                    spun.at[kk, :, g], spin_sem.at[kk, g],
                ))
        for move in moves:
            move.start()
        for move in moves:
            move.wait()
        spun_other[...] = spun[1].astype(BF16)
        spin_give().start()
        rotated[...] = spun[0].astype(BF16)
        order_wait()

        for level in range(levels):
            for kk in range(2):
                for kc in range(2):
                    @pl.when(is_source(kc))
                    def _():
                        for i in range(fan):
                            row_out(kc, level, kk, i).wait_send()

                    @pl.when(is_relay(kc))
                    def _():
                        row_relay(kc, level, kk).wait_send()

                row_give(level, kk).wait_send()
                for d in range(col_count):
                    @pl.when(jnp.logical_or(level != z, kk == 0))
                    def _():
                        across(level, kk, d).wait_send()

        for o in range(levels):
            for kk in range(2):
                for d in range(col_count):
                    @pl.when(jnp.logical_and(not_top, z - o >= 0))
                    def _():
                        up(o, kk, d).wait_send()

                    @pl.when(jnp.logical_and(not_bottom, z + o <= levels - 1))
                    def _():
                        down(o, kk, d).wait_send()

        for d in range(1, levels):
            sum_copy(d).wait_send()
        spin_give().wait_send()
        left_in().wait_recv()
        right_copy().wait_recv()
        ends_copy().wait_recv()

    def left_in():
        return remote(right.at[0], left, end_send.at[0, 0], end_recv.at[0], (r, c))

    def right_copy():
        return remote(right, right, end_send.at[2, 0], end_recv.at[1], sib)

    def ends_copy():
        return remote(ends, ends, end_send.at[2, 1], end_recv.at[2], sib)

    def main_core():
        for d in order:
            if d != 0:
                first_in(back(d)).wait_recv()
            across(z, 1, d).start()
        eig_copy().start()
        for d in order:
            across(z, 0, d).wait_recv()

        def lead_z(d):
            place = lead_all.at[z]
            return remote(place, place, leadz_send.at[d], leadz_recv.at[d], along(d))

        def lead_z_in(d):
            place = lead_all.at[lax.rem(z + levels - d, levels)]
            return remote(place, place, leadz_send.at[d], leadz_recv.at[d], along(d))

        def lead_plane(d, q):
            level = lax.rem(z + levels - d, levels)
            place = lead_all.at[level]
            return remote(place, place, leadp_send.at[d, q], leadp_recv.at[level], (r, q))

        def lead_in(level):
            place = lead_all.at[level]
            return remote(place, place, leadp_send.at[0, 0], leadp_recv.at[level], (r, c))

        @pl.when(c == 0)
        def _():
            for kk in range(2):
                for a in range(2):
                    block = col_all[a, z, kk, :, :, 0:tile].astype(F32).reshape(deep, tile)
                    lead_all[z, kk, a] = jnp.transpose(block)[0:LEAD].astype(BF16)
            for q in range(1, col_count):
                lead_plane(0, q).start()
            for d in range(1, levels):
                lead_z(d).start()

        def absorb_own(level):
            for kk in range(2):
                at = pl.multiple_of((level * 2 + kk) * deep, deep)
                for a in range(2):
                    own = col_all[a, level, kk].reshape(deep, full)
                    natural[a, pl.ds(at, deep), 0:full] = own
                    turned[a, :, pl.ds(at, deep)] = jnp.transpose(own.astype(F32)).astype(BF16)

        def absorb_lead(level):
            for kk in range(2):
                at = pl.multiple_of((level * 2 + kk) * deep, deep)
                for a in range(2):
                    lead = lead_all[level, kk, a].astype(F32)
                    lead = jnp.concatenate(
                        [lead, jnp.zeros((tile - LEAD, deep), F32)], axis=0
                    )
                    natural[a, pl.ds(at, deep), full:wide] = jnp.transpose(lead).astype(BF16)

        def absorb(level):
            for kk in range(2):
                for d in range(col_count):
                    across(level, kk, d).wait_recv()
            absorb_own(level)
            absorb_lead(level)

        def lead_product(level):
            total = jnp.zeros((LEAD, wide), F32)
            for kk in range(2):
                at = pl.multiple_of((level * 2 + kk) * deep, deep)
                for a in range(2):
                    total = total + jnp.dot(
                        lead_all[level, kk, a], natural[1 - a, pl.ds(at, deep), :],
                        preferred_element_type=F32,
                    )
            return 0.5 * total

        absorb_own(z)

        @pl.when(c != 0)
        def _():
            lead_in(z).wait_recv()

        absorb_lead(z)
        partial[...] = lead_product(z)
        vw[...] = jnp.zeros_like(vw)
        ends[...] = jnp.zeros_like(ends)

        lane = lax.broadcasted_iota(jnp.int32, (1, wide), 1)
        own_tile = lax.div(lane, tile)
        inside = lane - own_tile * tile
        parity = lax.div(own_tile, row_tiles)
        band = c + col_count * parity + row_count * (own_tile - row_tiles * parity)
        pos = jnp.where(lane < full, band * tile + inside, lane - full)
        lane1 = lax.broadcasted_iota(jnp.int32, (1, tile), 1)
        lane2 = lax.broadcasted_iota(jnp.int32, (2 * PB, tile), 1)
        sub2 = lax.broadcasted_iota(jnp.int32, (2 * PB, tile), 0)
        sub8 = lax.broadcasted_iota(jnp.int32, (8, full), 0)
        sub1 = lax.broadcasted_iota(jnp.int32, (8, 1), 0)
        zwidth = 2 * wide + tile

        def swap(column):
            return jnp.concatenate([column[PB:], column[:PB]], axis=0)

        def zcopies(slot):
            return [
                remote(
                    zoutgoing.at[slot, pl.ds(0, 1)], zmessage.at[slot, pl.ds(z, 1)],
                    zmsg_send.at[slot, d], zmsg_recv.at[slot, d], along(d),
                )
                for d in range(1, levels)
            ]

        def zsum(slot, pieces):
            mine = jnp.concatenate(pieces, axis=1)
            zoutgoing[slot, 0:1, :] = mine
            copies = zcopies(slot)
            for copy in copies:
                copy.start()
            for copy in copies:
                copy.wait()
            return rows_sum(zmessage[slot] + jnp.where(sub1 == z, mine, 0.0))

        opening = zsum(2, [partial[0:1, :], partial[1:2, :], jnp.zeros((1, tile), F32)])
        panel[0:1, :] = opening[:, :wide]
        panel[1:2, :] = opening[:, wide : 2 * wide]

        def front(step):
            both = vw[...]
            lead_vw = both[:, full:]
            head = lanes_sum(jnp.where(lane2 == step, lead_vw, 0.0))
            column = panel[pl.ds(step, 1), :] - rows_sum(both * swap(head))
            masked = jnp.where(pos > step + 1, column, 0.0)[:, :full]
            high, middle, low = parts_of(masked)
            stacked = jnp.where(
                sub8 == 0, high, jnp.where(sub8 == 1, middle, jnp.where(sub8 == 2, low, 0.0))
            ).astype(BF16)
            return both, column, masked, stacked

        def smalls(both, masked):
            onto = lanes_sum(both[:, :full] * masked)
            tail = lanes_sum(masked * masked)
            return rows_sum(jnp.where(lane2 == sub2, onto, 0.0)) + jnp.where(
                lane1 == 2 * PB, tail, 0.0
            )

        def plane_copies(slot, at):
            return [
                remote(
                    outgoing.at[slot, pl.ds(0, 1), at:], message.at[slot, pl.ds(c, 1), at:],
                    msg_send.at[slot, d], msg_recv.at[slot, d],
                    (r, lax.rem(c + d, col_count)),
                )
                for d in range(1, col_count)
            ]

        def settle(step, both, column, product, square, small):
            lead_column = column[:, full:]
            pivot = lanes_sum(jnp.where(lane1 == step + 1, lead_column, 0.0))
            here = lanes_sum(jnp.where(lane1 == step, lead_column, 0.0))
            next_row = panel[pl.ds(step + 1, 1), :]
            corner = lanes_sum(jnp.where(lane1 == step + 1, next_row[:, full:], 0.0))
            head_next = lanes_sum(jnp.where(lane2 == step + 1, both[:, full:], 0.0))
            tail = lanes_sum(jnp.where(lane1 == 2 * PB, small, 0.0))
            onto = lanes_sum(jnp.where(lane2 == sub2, small, 0.0))
            length = jnp.sqrt(pivot * pivot + tail)
            beta = jnp.where(pivot >= 0.0, -length, length)
            tau = (beta - pivot) / beta
            inverse = 1.0 / (pivot - beta)
            vector = jnp.where(
                pos == step + 1, 1.0, jnp.where(pos > step + 1, column * inverse, 0.0)
            )
            onto = onto * inverse + head_next
            image = tau * (product * inverse + next_row - rows_sum(both * swap(onto)))
            edge = lanes_sum(jnp.where(lane1 == step + 1, product[:, full:], 0.0))
            energy = square * inverse * inverse + 2.0 * inverse * edge + corner
            overlap = tau * (energy - 2.0 * rows_sum(onto[:PB] * onto[PB:]))
            image = image - 0.5 * tau * overlap * vector
            vw[pl.ds(step, 1), :] = vector
            vw[pl.ds(PB + step, 1), :] = image
            ends[0:1, :] = jnp.where(lane1 == step, here, ends[0:1, :])
            ends[1:2, :] = jnp.where(lane1 == step, beta, ends[1:2, :])

        def pieces_of(sums):
            return jnp.concatenate(
                parts_of(sums) + (jnp.zeros_like(sums),), axis=0
            ).astype(BF16)

        near = pl.multiple_of(z * pair, pair)
        early_at = 2 * gvecs - 2 * pair

        def early_background(step):
            @pl.when(step == 0)
            def _():
                @pl.when(c == 0)
                def _():
                    for d in range(1, levels):
                        lead_z_in(d).wait_recv()
                        for q in range(1, col_count):
                            lead_plane(d, q).start()

            @pl.when(step == 2)
            def _():
                @pl.when(c != 0)
                def _():
                    for d in range(1, levels):
                        lead_in(lax.rem(z + d, levels)).wait_recv()

                @pl.when(z >= 1)
                def _():
                    absorb(z - 1)

            @pl.when(step == 3)
            def _():
                @pl.when(z + 1 <= levels - 1)
                def _():
                    absorb(z + 1)

        @pl.loop(0, EARLY)
        def _(step):
            slot = lax.rem(step, 2)
            both, column, masked, stacked = front(step)
            mine = []
            for a in range(2):
                mine.append(rows_sum(jnp.dot(
                    stacked, turned[a, :, pl.ds(near, pair)], preferred_element_type=F32
                )))
            mine.append(smalls(both, masked))
            mine = jnp.concatenate(mine, axis=1)
            outgoing[slot, 0:1, early_at:] = mine
            copies = plane_copies(slot, early_at)
            for copy in copies:
                copy.start()
            early_background(step)
            for copy in copies:
                copy.wait()
            received = message[slot, :, early_at:] + jnp.where(sub1 == c, mine, 0.0)
            sums = received[:, : 2 * pair]
            pieces = pieces_of(sums)
            product = 0.5 * rows_sum(
                jnp.dot(
                    pieces[:, :pair], natural[1, pl.ds(near, pair), :],
                    preferred_element_type=F32,
                )
                + jnp.dot(
                    pieces[:, pair:], natural[0, pl.ds(near, pair), :],
                    preferred_element_type=F32,
                )
            )
            whole_sum = rows_sum(sums)
            square = lanes_sum(whole_sum[:, :pair] * whole_sum[:, pair:])
            small = rows_sum(received[:, 2 * pair :])
            total = zsum(slot, [
                product, partial[pl.ds(step + 2, 1), :], jnp.where(lane1 == 0, square, 0.0),
            ])
            panel[pl.ds(step + 2, 1), :] = total[:, wide : 2 * wide]
            square = lanes_sum(total[:, 2 * wide :])
            settle(step, both, column, total[:, :wide], square, small)

        for o in range(1, levels - 1):
            @pl.when(z - 1 - o >= 0)
            def _():
                absorb(z - 1 - o)

            @pl.when(z + 1 + o <= levels - 1)
            def _():
                absorb(z + 1 + o)

        start = lead_product(0)
        for level in range(1, levels):
            start = start + lead_product(level)
        panel[...] = start

        rows_at = EARLY + 3
        work_at = rows_at + 1

        def background(step):
            @pl.when(step == rows_at)
            def _():
                for level in range(levels):
                    for kk in range(2):
                        row_give(level, kk).wait_recv()

            @pl.when(jnp.logical_and(step >= work_at, step < work_at + row_tiles))
            def _():
                block_work(2 * (step - work_at), 1)
                block_work(2 * (step - work_at) + 1, 1)

            @pl.when(step == work_at + row_tiles)
            def _():
                order_start()

            @pl.when(step == PB - 1)
            def _():
                order_wait()

        @pl.loop(EARLY, PB)
        def _(step):
            slot = lax.rem(step, 2)
            both, column, masked, stacked = front(step)
            mine = []
            for a in range(2):
                mine.append(
                    rows_sum(jnp.dot(stacked, turned[a], preferred_element_type=F32))
                )
            mine.append(smalls(both, masked))
            mine = jnp.concatenate(mine, axis=1)
            outgoing[slot, 0:1, :] = mine
            copies = plane_copies(slot, 0)
            for copy in copies:
                copy.start()
            background(step)
            for copy in copies:
                copy.wait()
            received = message[slot] + jnp.where(sub1 == c, mine, 0.0)
            sums = received[:, : 2 * gvecs]
            pieces = pieces_of(sums)
            product = 0.5 * rows_sum(
                jnp.dot(pieces[:, :gvecs], natural[1], preferred_element_type=F32)
                + jnp.dot(pieces[:, gvecs:], natural[0], preferred_element_type=F32)
            )
            whole_sum = rows_sum(sums)
            square = lanes_sum(whole_sum[:, :gvecs] * whole_sum[:, gvecs:])
            settle(step, both, column, product, square, rows_sum(received[:, 2 * gvecs :]))

        for side in range(2):
            right[side] = vw[:, side * half : (side + 1) * half]

        def left_out(kc, q):
            return remote(
                right.at[source_half(kc)], left, end_send.at[kc, q], end_recv.at[0],
                (2 * z + kc, q),
            )

        def each_left(action):
            for kc in range(2):
                for q in range(col_count):
                    away = c == source_c(kc)
                    if kc == 1:
                        away = jnp.logical_and(away, c != q)

                    @pl.when(away)
                    def _():
                        action(left_out(kc, q))

        each_left(lambda copy: copy.start())
        right_copy().start()
        ends_copy().start()

        @pl.when(c == source_c(1))
        def _():
            left[...] = right[source_half(1)]

        @pl.when(c != source_c(1))
        def _():
            left_in().wait_recv()

        each_left(lambda copy: copy.wait_send())
        right_copy().wait_send()
        ends_copy().wait_send()
        spin_give().wait_recv()
        eig_copy().wait_send()
        for d in range(col_count):
            across(z, 1, d).wait_send()

        @pl.when(c == 0)
        def _():
            for d in range(levels):
                for q in range(1, col_count):
                    lead_plane(d, q).wait_send()
            for d in range(1, levels):
                lead_z(d).wait_send()

    for d in range(1, col_count):
        first(d).start()

    @pl.when(k == 0)
    def _():
        helper_core()

    @pl.when(is_main)
    def _():
        main_core()

    for d in range(1, col_count):
        first(d).wait_send()


def step(psi, hpsi, eig, sizes):
    row_count, col_count, row_tiles, col_tiles, tile = sizes
    g_rows = psi.shape[0]
    half = row_tiles * tile
    full = col_tiles * tile
    wide = full + tile
    levels = row_count // 2
    gvecs = row_count * col_count * g_rows
    deep = gvecs // row_count
    whole = pl.BlockSpec(memory_space=pltpu.VMEM)
    dma = pltpu.SemaphoreType.DMA

    def both(*shape):
        return [dma(shape), dma(shape)]

    return pl.pallas_call(
        functools.partial(step_kernel, sizes),
        out_shape=(
            jax.ShapeDtypeStruct((half, full), F32),
            jax.ShapeDtypeStruct((half, col_tiles, tile), F32),
            jax.ShapeDtypeStruct((2 * PB, half), F32),
            jax.ShapeDtypeStruct((2, 2 * PB, half), F32),
            jax.ShapeDtypeStruct((8, tile), F32),
            jax.ShapeDtypeStruct((deep, col_tiles, tile), BF16),
        ),
        in_specs=[whole] * 3,
        out_specs=(whole,) * 6,
        scratch_shapes=[
            pltpu.VMEM((half, full), F32),
            pltpu.VMEM((2, levels, 2, col_count, g_rows, full), BF16),
            pltpu.VMEM((2, 2, levels, 2, col_count, g_rows, half), BF16),
            pltpu.VMEM((levels, 2, 2, LEAD, deep), BF16),
            pltpu.VMEM((col_count, 2, g_rows, full), BF16),
            pltpu.VMEM((2, gvecs, wide), BF16),
            pltpu.VMEM((2, full, gvecs), BF16),
            pltpu.VMEM((LEAD, wide), F32),
            pltpu.VMEM((LEAD, wide), F32),
            pltpu.VMEM((2 * PB, wide), F32),
            pltpu.VMEM((2, 8, 2 * gvecs + tile), F32),
            pltpu.VMEM((2, 8, 2 * gvecs + tile), F32),
            pltpu.VMEM((3, 8, 2 * wide + tile), F32),
            pltpu.VMEM((3, 8, 2 * wide + tile), F32),
            pltpu.VMEM((half, full), BF16),
            pltpu.VMEM((levels, 2 * deep, full), F32),
            pltpu.VMEM((levels, 2 * deep, full), F32),
            pltpu.VMEM((2, deep, col_tiles, tile), F32),
            pltpu.VMEM((deep, col_tiles, tile), BF16),
            *both(col_count),
            *both(levels, 2, col_count), *both(levels, 2, col_count),
            *both(levels, 2, col_count),
            *both(levels),
            dma((levels, col_count)), dma((levels,)),
            dma((2, levels, 2, col_count // 2)), dma((2, levels, 2)), dma((2, levels, 2)),
            *both(levels, 2),
            *both(2, col_count), *both(3, levels),
            dma((3, col_count)), dma((3,)),
            *both(1), *both(levels),
            dma((2, col_tiles)), dma((col_tiles,)),
            *both(1),
        ],
        compiler_params=pltpu.CompilerParams(
            collective_id=0, has_side_effects=True, vmem_limit_bytes=60 * 1024 * 1024
        ),
        cost_estimate=pl.CostEstimate(
            flops=400_000_000, bytes_accessed=4_000_000, transcendentals=0
        ),
        name="step",
    )(psi, hpsi, eig)


def finish_kernel(
    sizes, reduced, correlation, left, right, ends, rotated,
    updated_out, corr_out, diag_out, off_out, rotated_out, updated, sems,
):
    row_count, col_count, row_tiles, col_tiles, tile = sizes

    def place(position):
        return 2 * (position % row_tiles) + position // row_tiles

    spin = pltpu.make_async_copy(rotated, rotated_out, sems.at[0])
    spin.start()
    diag_out[...] = ends[0:1, :PB]
    off_out[...] = ends[1:2, :PB]
    first = pltpu.make_async_copy(correlation, corr_out, sems.at[1])
    first.start()
    moves = [spin, first]
    high, middle, low = parts_of(left[...])
    lhs = jnp.concatenate([high, high, middle, middle, high, low], axis=0).astype(BF16)
    for parity in range(2):
        other = right[parity]
        other = jnp.concatenate([other[PB:], other[:PB]], axis=0)
        high, middle, low = parts_of(other)
        rhs = jnp.concatenate([high, middle, high, middle, low, high], axis=0).astype(BF16)
        width = row_tiles * tile
        at = parity * width
        updated[:, at : at + width] = reduced[:, at : at + width] - inner(lhs, rhs)
        for t in range(row_tiles):
            position = parity * row_tiles + t
            move = pltpu.make_async_copy(
                updated.at[:, position * tile : (position + 1) * tile],
                updated_out.at[:, place(position)], sems.at[2 + position],
            )
            move.start()
            moves.append(move)
    for move in moves:
        move.wait()


def finish(parts, sizes):
    row_count, col_count, row_tiles, col_tiles, tile = sizes
    whole = pl.BlockSpec(memory_space=pltpu.VMEM)
    hbm = pl.BlockSpec(memory_space=pl.ANY)
    shape = (row_tiles * tile, col_tiles, tile)
    return pl.pallas_call(
        functools.partial(finish_kernel, sizes),
        out_shape=(
            jax.ShapeDtypeStruct(shape, F32), jax.ShapeDtypeStruct(shape, F32),
            jax.ShapeDtypeStruct((1, PB), F32), jax.ShapeDtypeStruct((1, PB), F32),
            jax.ShapeDtypeStruct(parts[-1].shape, BF16),
        ),
        in_specs=[whole] * 6,
        out_specs=(hbm, hbm, whole, whole, hbm),
        scratch_shapes=[
            pltpu.VMEM((row_tiles * tile, col_tiles * tile), F32),
            pltpu.SemaphoreType.DMA((2 + col_tiles,)),
        ],
        cost_estimate=pl.CostEstimate(
            flops=200_000_000, bytes_accessed=8_000_000, transcendentals=0
        ),
        name="finish",
    )(*parts)


def on_device(psi, hpsi, eigvec):
    row_tiles = eigvec.shape[0]
    tile = eigvec.shape[2]
    col_tiles = eigvec.shape[3]
    row_count = lax.axis_size("row")
    col_count = lax.axis_size("col")
    sizes = (row_count, col_count, row_tiles, col_tiles, tile)
    flat = eigvec.reshape(row_tiles * tile, col_tiles * tile)
    parts = step(psi, hpsi, flat, sizes)
    updated, correlation, diagonal, offdiag, rotated = finish(parts, sizes)
    tile_shape = (row_tiles, 1, tile, col_tiles, 1, tile)
    return (
        correlation.reshape(tile_shape),
        updated.reshape(tile_shape),
        diagonal.reshape(PB),
        offdiag.reshape(PB),
        rotated.reshape(rotated.shape[0], col_tiles, 1, tile),
    )


def solution(mesh):
    return jax.shard_map(
        on_device,
        mesh=mesh,
        in_specs=(
            P(("row", "col"), None),
            P(("row", "col"), None),
            P(None, "row", None, None, "col", None),
        ),
        out_specs=(
            P(None, "row", None, None, "col", None),
            P(None, "row", None, None, "col", None),
            P(),
            P(),
            P("row", None, "col", None),
        ),
        check_vma=False,
    )
```

time: 140 us -> 125 us (0.89)
  Pallas kernels: 135 us -> 121 us
    pallas_call x1, Pallas kernels: 130 us -> 116 us  [step(): pl.pallas_call(functools.partial(step_kernel, sizes), out_shape=(jax.Shap...]
    unnamed x8 -> x1, local copies, waits for them, and re-layouts: 3.19 us -> 2.47 us
where the time goes in v3:
time: 125 us; the launch traced here: 124 us
  Pallas kernels  121 us (97%)
  local copies, waits for them, and re-layouts  2.47 us (2%)
    pallas_call x1, Pallas kernels, step(): pl.pallas_call(functools.partial(step_kernel, sizes), out_shape=(jax.Shap...  116 us
    pallas_call x1, Pallas kernels, finish(): pl.pallas_call(functools.partial(finish_kernel, sizes), out_shape=(jax.Sh...  4.96 us

profile of v3, /device:TPU:0, one launch (start us, length us, event | category | flops | bytes accessed | tf_op | source)
XLA Modules:
  0.0 123.8 jit_solution(15789908755306921752)
XLA Ops:
  0.6 2.5 %copy.13 = bf16[64,8,8,128]{3,1,2,0:T(8,128)(2,1)} copy(bf16[64,8,8,128]{3,2,1,0:T(8,128)(2,1)} %bitcast.18) | data formatting | bytes 2097152
  3.1 115.5 %step.1 = (f32[512,1024]{1,0:T(8,128)}, f32[512,8,128]{2,1,0:T(8,128)}, f32[32,512]{1,0:T(8,128)}, f32[2,32,512]{2,1,0:T(8,128)}, f32[8,128]{1,0:T(8,128)}, /*index=5*/bf16[128,8,128]{2,1,0:T(8,128)(2,1)}) custom-call(bf16[32,4096]{1,0:T(8,128)(2,1)} %psi.1, bf16[32,4096]{1,0:T(8,128)(2,1)} %hpsi.1, bf16[512,1024]{1,0:T(8,128)(2,1)} %bitcast.17), custom_call_target="tpu_custom_call" | custom-call | flops 400000000 | bytes 4000000 | tf_op jit(solution)/shard_map/step/pallas_call | solution.py:818
  118.7 5.0 %finish.1 = (f32[512,8,128]{2,1,0:T(8,128)}, f32[512,8,128]{2,1,0:T(8,128)}, f32[1,16]{1,0:T(1,128)}, f32[1,16]{1,0:T(1,128)}, bf16[128,8,128]{2,1,0:T(8,128)(2,1)}) custom-call(f32[512,1024]{1,0:T(8,128)} %get-tuple-element.16.reduced, f32[512,8,128]{2,1,0:T(8,128)} %get-tuple-element.17.correlation, f32[32,512]{1,0:T(8,128)} %get-tuple-element.18.left, ...), custom_call_target="tpu_custom_call" | custom-call | flops 200000000 | bytes 8000000 | tf_op jit(solution)/shard_map/finish/pallas_call | solution.py:916

commit v4 on v3

--- a/solution.py
+++ b/solution.py
@@ -1,4 +1,5 @@
 import functools
+import math
 
 import jax
 import jax.numpy as jnp
@@ -27,13 +28,6 @@
     )
 
 
-def enter(devices):
-    barrier = pltpu.get_barrier_semaphore()
-    for device in devices:
-        pl.semaphore_signal(barrier, inc=1, device_id=device, device_id_type=MESH)
-    pl.semaphore_wait(barrier, len(devices))
-
-
 def lanes_sum(array):
     return jnp.sum(array, axis=1, keepdims=True)
 
@@ -49,18 +43,18 @@
     return high, middle, rest - middle
 
 
-EARLY = 5
+EARLY = 4
 
 
 def step_kernel(
-    sizes, psi, hpsi, eig,
+    sizes, psi_in, hpsi_in, eig,
     reduced, ordered, left, right, ends, rotated,
-    correlation, col_all, row_all, lead_all, stage, natural, turned, panel, partial, vw,
-    message, outgoing, zmessage, zoutgoing, eig_other, keep, inbox, spun, spun_other,
+    psi, hpsi, col_all, row_all, lead_all, stage, natural, turned, panel, partial, vw,
+    message, outgoing, zmessage, zoutgoing, eig_raw, eig_flat, keep, inbox, spun, spun_other,
     s1_send, s1_recv, up_send, up_recv, down_send, down_recv, sib_send, sib_recv,
     leadz_send, leadz_recv, leadp_send, leadp_recv, row_send, row_recv, own_sem,
     give_send, give_recv, msg_send, msg_recv, zmsg_send, zmsg_recv,
-    end_send, end_recv, eig_send, eig_recv, sum_send, sum_recv, spin_sem, order_sem,
+    end_send, end_recv, eig_send, eig_recv, upsum_send, upsum_recv, downsum_send, downsum_recv, load_sem,
     spin_send, spin_recv,
 ):
     row_count, col_count, row_tiles, col_tiles, tile = sizes
@@ -96,6 +90,20 @@
 
     order = [0] + [back(d) for d in range(1, col_count)]
 
+    loads = [
+        pltpu.make_async_copy(psi_in, psi, load_sem.at[0]),
+        pltpu.make_async_copy(hpsi_in, hpsi, load_sem.at[1]),
+    ]
+    for load in loads:
+        load.start()
+    message[...] = jnp.zeros_like(message)
+    zmessage[...] = jnp.zeros_like(zmessage)
+    neighbours = [peer(d) for d in range(1, group)] + [along(d) for d in range(1, levels)]
+    barrier = pltpu.get_barrier_semaphore()
+    for device in neighbours:
+        pl.semaphore_signal(barrier, inc=1, device_id=device, device_id_type=MESH)
+    for load in loads:
+        load.wait()
     for target in range(col_count):
         for a, source in enumerate((psi, hpsi)):
             for parity in range(2):
@@ -104,9 +112,7 @@
                     at = (parity * row_tiles + t) * tile
                     stage[target, a, :, at : at + tile] = source[:, j * tile : (j + 1) * tile]
     col_all[:, z, k, c] = stage[c]
-    message[...] = jnp.zeros_like(message)
-    zmessage[...] = jnp.zeros_like(zmessage)
-    enter([peer(d) for d in range(1, group)] + [along(d) for d in range(1, levels)])
+    pl.semaphore_wait(barrier, len(neighbours))
 
     def first(d):
         return remote(
@@ -124,7 +130,7 @@
         )
 
     def eig_copy():
-        return remote(eig, eig_other, eig_send.at[0], eig_recv.at[0], sib)
+        return remote(eig, eig_raw.at[1], eig_send.at[0], eig_recv.at[0], sib)
 
     def row_give(level, kk):
         place = row_all.at[1, :, level, kk]
@@ -140,36 +146,23 @@
         return lax.div(2 * z + kc, col_count)
 
     def block_work(index, kc):
-        at = pl.multiple_of(lax.div(index, 2) * tile, tile)
-        to = pl.multiple_of(lax.rem(index, 2) * half, half)
+        at = pl.multiple_of(index * tile, tile)
 
         def rows_of(a):
             return row_all[kc, a, :, :, :, :, pl.ds(at, tile)].reshape(gvecs, tile)
 
-        def cols_of(a):
-            return col_all[a, :, :, :, :, pl.ds(to, half)].reshape(gvecs, half)
-
-        correlation[pl.ds(at, tile), pl.ds(to, half)] = inner(rows_of(0), cols_of(0)) * (
-            1.0 / gvecs
-        )
-        reduced[pl.ds(at, tile), pl.ds(to, half)] = 0.5 * (
-            inner(rows_of(0), cols_of(1)) + inner(rows_of(1), cols_of(0))
-        )
-
-    def order_copy(position):
-        return pltpu.make_async_copy(
-            correlation.at[:, position * tile : (position + 1) * tile],
-            ordered.at[:, 2 * (position % row_tiles) + position // row_tiles],
-            order_sem.at[position],
-        )
-
-    def order_start():
-        for position in range(col_tiles):
-            order_copy(position).start()
-
-    def order_wait():
-        for position in range(col_tiles):
-            order_copy(position).wait()
+        for side in range(2):
+            def cols_of(a):
+                return col_all[a, :, :, :, :, side * half : (side + 1) * half].reshape(
+                    gvecs, half
+                )
+
+            result = inner(rows_of(0), cols_of(0)) * (1.0 / gvecs)
+            for t in range(row_tiles):
+                ordered[pl.ds(at, tile), 2 * t + side, :] = result[:, t * tile : (t + 1) * tile]
+            reduced[pl.ds(at, tile), side * half : (side + 1) * half] = 0.5 * (
+                inner(rows_of(0), cols_of(1)) + inner(rows_of(1), cols_of(0))
+            )
 
     def helper_core():
         not_top = z < levels - 1
@@ -223,36 +216,43 @@
                 row_from(kc, level, kk), row_all.at[kc, :, level, kk], own_sem.at[kc, level, kk]
             )
 
-        def row_out(kc, level, kk, i):
+        def row_part(kc, level, kk, a):
+            lane0 = pl.multiple_of(source_half(kc) * half, half)
+            return col_all.at[a, level, kk, :, :, pl.ds(lane0, half)]
+
+        def row_out(kc, level, kk, a, i):
             device = (r, partner) if i == 0 else (r, lax.rem(c + 2 * i, col_count))
             return remote(
-                row_from(kc, level, kk), row_all.at[kc, :, level, kk],
-                row_send.at[kc, level, kk, i], row_recv.at[kc, level, kk], device,
-            )
-
-        def row_relay(kc, level, kk):
-            place = row_all.at[kc, :, level, kk]
+                row_part(kc, level, kk, a), row_all.at[kc, a, level, kk],
+                row_send.at[kc, level, kk, a, i], row_recv.at[kc, level, kk, a], device,
+            )
+
+        def row_relay(kc, level, kk, a):
+            place = row_all.at[kc, a, level, kk]
             return remote(
-                place, place, row_send.at[kc, level, kk, 0], row_recv.at[kc, level, kk],
-                (r, partner),
+                place, place, row_send.at[kc, level, kk, a, 0],
+                row_recv.at[kc, level, kk, a], (r, partner),
             )
 
         def row_launch(level):
             for kc in range(2):
                 @pl.when(is_source(kc))
                 def _():
+                    for a in range(2):
+                        for kk in range(2):
+                            for i in range(fan):
+                                row_out(kc, level, kk, a, i).start()
                     for kk in range(2):
-                        for i in range(fan):
-                            row_out(kc, level, kk, i).start()
                         row_own(kc, level, kk).start()
 
         def row_finish(level):
-            for kc in range(2):
-                @pl.when(is_relay(kc))
-                def _():
-                    for kk in range(2):
-                        row_relay(kc, level, kk).wait_recv()
-                        row_relay(kc, level, kk).start()
+            for a in range(2):
+                for kk in range(2):
+                    for kc in range(2):
+                        @pl.when(is_relay(kc))
+                        def _():
+                            row_relay(kc, level, kk, a).wait_recv()
+                            row_relay(kc, level, kk, a).start()
 
         for d in order:
             if d != 0:
@@ -262,6 +262,14 @@
             across(z, 1, d).wait_recv()
             launch(1, d)
         row_launch(z)
+        own_eig = pltpu.make_async_copy(eig, eig_raw.at[0], load_sem.at[0])
+        own_eig.start()
+        own_eig.wait()
+        eig_copy().wait_recv()
+        for kc in range(2):
+            values = eig_raw[kc].astype(F32)
+            for g in range(col_tiles):
+                eig_flat[kc, :, g * tile : (g + 1) * tile] = values[:, g, :].astype(BF16)
         for o in range(levels - 1):
             below = z - 1 - o >= 0
             above = z + 1 + o <= levels - 1
@@ -314,6 +322,14 @@
         def _():
             row_finish(z + levels - 1)
 
+        def row_wait(a):
+            for level in range(levels):
+                for kk in range(2):
+                    for kc in range(2):
+                        @pl.when(jnp.logical_not(jnp.logical_or(is_source(kc), is_relay(kc))))
+                        def _():
+                            row_relay(kc, level, kk, a).wait_recv()
+
         for level in range(levels):
             for kk in range(2):
                 for kc in range(2):
@@ -321,67 +337,124 @@
                     def _():
                         row_own(kc, level, kk).wait()
 
-                    @pl.when(jnp.logical_not(jnp.logical_or(is_source(kc), is_relay(kc))))
-                    def _():
-                        row_relay(kc, level, kk).wait_recv()
-
+        row_wait(0)
+
+        def upsum(level):
+            return remote(
+                keep.at[level], inbox.at[level], upsum_send.at[level], upsum_recv.at[level],
+                (r + 2, c),
+            )
+
+        def downsum(level, place):
+            return remote(
+                keep.at[level], inbox.at[place], downsum_send.at[level],
+                downsum_recv.at[level], (r - 2, c),
+            )
+
+        def partial_sum(level):
+            keep[level] = jnp.dot(
+                row_all[0, 0, level].reshape(pair, half), eig_flat[0],
+                preferred_element_type=F32,
+            ) + jnp.dot(
+                row_all[1, 0, level].reshape(pair, half), eig_flat[1],
+                preferred_element_type=F32,
+            )
+
+        def send_down(level):
+            @pl.when(z - 1 == level)
+            def _():
+                downsum(level, levels).start()
+
+            @pl.when(z - 1 != level)
+            def _():
+                downsum(level, level).start()
+
+        for i in range(levels - 1):
+            high, low = levels - 1 - i, i
+
+            @pl.when(z < high)
+            def _():
+                partial_sum(high)
+
+                @pl.when(z == 0)
+                def _():
+                    upsum(high).start()
+
+            @pl.when(z > low)
+            def _():
+                partial_sum(low)
+
+                @pl.when(z == levels - 1)
+                def _():
+                    send_down(low)
+
+        partial_sum(z)
+        row_wait(1)
+        for level in range(levels):
+            for kk in range(2):
                 row_give(level, kk).start()
-        eig_copy().wait_recv()
-
-        def sum_copy(d):
-            return remote(
-                keep.at[lax.rem(z + d, levels)], inbox.at[d], sum_send.at[d], sum_recv.at[d],
-                along(d),
-            )
-
-        for i in range(levels):
-            level = lax.rem(z + 1 + i, levels)
-            keep[level] = jnp.dot(
-                row_all[0, 0, level].reshape(pair, half), eig[...], preferred_element_type=F32
-            ) + jnp.dot(
-                row_all[1, 0, level].reshape(pair, half), eig_other[...],
-                preferred_element_type=F32,
-            )
-            if i < levels - 1:
-                sum_copy(i + 1).start()
-
-        @pl.loop(0, 2 * row_tiles)
+
+        @pl.loop(0, row_tiles)
         def _(index):
             block_work(index, 0)
 
-        order_start()
-        result = keep[z]
-        for d in range(1, levels):
-            sum_copy(d).wait_recv()
-            result = result + inbox[d]
-        inbox[0] = result
-        moves = []
-        for kk in range(2):
+        def pass_up(high):
+            @pl.when(jnp.logical_and(z > 0, z < high))
+            def _():
+                upsum(high).wait_recv()
+                keep[high] = keep[high] + inbox[high]
+                upsum(high).start()
+
+        def pass_down(low):
+            @pl.when(jnp.logical_and(z < levels - 1, z > low))
+            def _():
+                downsum(low, low).wait_recv()
+                keep[low] = keep[low] + inbox[low]
+                send_down(low)
+
+        @pl.when(z < levels // 2)
+        def _():
+            for i in range(levels - 1):
+                pass_up(levels - 1 - i)
+                pass_down(i)
+
+        @pl.when(z >= levels // 2)
+        def _():
+            for i in range(levels - 1):
+                pass_down(i)
+                pass_up(levels - 1 - i)
+
+        @pl.when(z > 0)
+        def _():
+            upsum(z).wait_recv()
+            keep[z] = keep[z] + inbox[z]
+
+        @pl.when(z < levels - 1)
+        def _():
+            downsum(z, levels).wait_recv()
+            keep[z] = keep[z] + inbox[levels]
+
+        for kk in (1, 0):
             for g in range(col_tiles):
-                moves.append(pltpu.make_async_copy(
-                    inbox.at[0, kk * deep : (kk + 1) * deep, g * tile : (g + 1) * tile],
-                    spun.at[kk, :, g], spin_sem.at[kk, g],
-                ))
-        for move in moves:
-            move.start()
-        for move in moves:
-            move.wait()
-        spun_other[...] = spun[1].astype(BF16)
-        spin_give().start()
-        rotated[...] = spun[0].astype(BF16)
-        order_wait()
+                spun[:, g, :] = keep[z, kk * deep : (kk + 1) * deep, g * tile : (g + 1) * tile]
+            if kk:
+                spun_other[...] = spun[...].astype(BF16)
+                spin_give().start()
+            else:
+                rotated[...] = spun[...].astype(BF16)
 
         for level in range(levels):
             for kk in range(2):
                 for kc in range(2):
-                    @pl.when(is_source(kc))
-                    def _():
-                        for i in range(fan):
-                            row_out(kc, level, kk, i).wait_send()
-
-                    @pl.when(is_relay(kc))
-                    def _():
-                        row_relay(kc, level, kk).wait_send()
+                    for a in range(2):
+                        @pl.when(is_source(kc))
+                        def _():
+                            for i in range(fan):
+                                row_out(kc, level, kk, a, i).wait_send()
+
+                        @pl.when(is_relay(kc))
+                        def _():
+                            row_relay(kc, level, kk, a).wait_send()
 
                 row_give(level, kk).wait_send()
                 for d in range(col_count):
@@ -400,8 +473,15 @@
                     def _():
                         down(o, kk, d).wait_send()
 
-        for d in range(1, levels):
-            sum_copy(d).wait_send()
+        for level in range(levels):
+            @pl.when(z < level)
+            def _():
+                upsum(level).wait_send()
+
+            @pl.when(z > level)
+            def _():
+                downsum(level, level).wait_send()
+
         spin_give().wait_send()
         left_in().wait_recv()
         right_copy().wait_recv()
@@ -685,7 +765,7 @@
             start = start + lead_product(level)
         panel[...] = start
 
-        rows_at = EARLY + 3
+        rows_at = EARLY + 4
         work_at = rows_at + 1
 
         def background(step):
@@ -697,16 +777,7 @@
 
             @pl.when(jnp.logical_and(step >= work_at, step < work_at + row_tiles))
             def _():
-                block_work(2 * (step - work_at), 1)
-                block_work(2 * (step - work_at) + 1, 1)
-
-            @pl.when(step == work_at + row_tiles)
-            def _():
-                order_start()
-
-            @pl.when(step == PB - 1)
-            def _():
-                order_wait()
+                block_work(step - work_at, 1)
 
         @pl.loop(EARLY, PB)
         def _(step):
@@ -815,6 +886,45 @@
     def both(*shape):
         return [dma(shape), dma(shape)]
 
+    scratch = [
+        pltpu.VMEM((g_rows, psi.shape[1]), BF16),
+        pltpu.VMEM((g_rows, psi.shape[1]), BF16),
+        pltpu.VMEM((2, levels, 2, col_count, g_rows, full), BF16),
+        pltpu.VMEM((2, 2, levels, 2, col_count, g_rows, half), BF16),
+        pltpu.VMEM((levels, 2, 2, LEAD, deep), BF16),
+        pltpu.VMEM((col_count, 2, g_rows, full), BF16),
+        pltpu.VMEM((2, gvecs, wide), BF16),
+        pltpu.VMEM((2, full, gvecs), BF16),
+        pltpu.VMEM((LEAD, wide), F32),
+        pltpu.VMEM((LEAD, wide), F32),
+        pltpu.VMEM((2 * PB, wide), F32),
+        pltpu.VMEM((2, 8, 2 * gvecs + tile), F32),
+        pltpu.VMEM((2, 8, 2 * gvecs + tile), F32),
+        pltpu.VMEM((3, 8, 2 * wide + tile), F32),
+        pltpu.VMEM((3, 8, 2 * wide + tile), F32),
+        pltpu.VMEM((2, half, col_tiles, tile), BF16),
+        pltpu.VMEM((2, half, full), BF16),
+        pltpu.VMEM((levels, 2 * deep, full), F32),
+        pltpu.VMEM((levels + 1, 2 * deep, full), F32),
+        pltpu.VMEM((deep, col_tiles, tile), F32),
+        pltpu.VMEM((deep, col_tiles, tile), BF16),
+        *both(col_count),
+        *both(levels, 2, col_count), *both(levels, 2, col_count),
+        *both(levels, 2, col_count),
+        *both(levels),
+        dma((levels, col_count)), dma((levels,)),
+        dma((2, levels, 2, 2, col_count // 2)), dma((2, levels, 2, 2)),
+        dma((2, levels, 2)),
+        *both(levels, 2),
+        *both(2, col_count), *both(3, levels),
+        dma((3, col_count)), dma((3,)),
+        *both(1), *both(levels), *both(levels), dma((2,)),
+        *both(1),
+    ]
+    held = sum(
+        math.prod(item.shape) * jnp.dtype(item.dtype).itemsize
+        for item in scratch if item.memory_space == pltpu.VMEM
+    )
     return pl.pallas_call(
         functools.partial(step_kernel, sizes),
         out_shape=(
@@ -825,43 +935,11 @@
             jax.ShapeDtypeStruct((8, tile), F32),
             jax.ShapeDtypeStruct((deep, col_tiles, tile), BF16),
         ),
-        in_specs=[whole] * 3,
+        in_specs=[pl.BlockSpec(memory_space=pltpu.HBM)] * 3,
         out_specs=(whole,) * 6,
-        scratch_shapes=[
-            pltpu.VMEM((half, full), F32),
-            pltpu.VMEM((2, levels, 2, col_count, g_rows, full), BF16),
-            pltpu.VMEM((2, 2, levels, 2, col_count, g_rows, half), BF16),
-            pltpu.VMEM((levels, 2, 2, LEAD, deep), BF16),
-            pltpu.VMEM((col_count, 2, g_rows, full), BF16),
-            pltpu.VMEM((2, gvecs, wide), BF16),
-            pltpu.VMEM((2, full, gvecs), BF16),
-            pltpu.VMEM((LEAD, wide), F32),
-            pltpu.VMEM((LEAD, wide), F32),
-            pltpu.VMEM((2 * PB, wide), F32),
-            pltpu.VMEM((2, 8, 2 * gvecs + tile), F32),
-            pltpu.VMEM((2, 8, 2 * gvecs + tile), F32),
-            pltpu.VMEM((3, 8, 2 * wide + tile), F32),
-            pltpu.VMEM((3, 8, 2 * wide + tile), F32),
-            pltpu.VMEM((half, full), BF16),
-            pltpu.VMEM((levels, 2 * deep, full), F32),
-            pltpu.VMEM((levels, 2 * deep, full), F32),
-            pltpu.VMEM((2, deep, col_tiles, tile), F32),
-            pltpu.VMEM((deep, col_tiles, tile), BF16),
-            *both(col_count),
-            *both(levels, 2, col_count), *both(levels, 2, col_count),
-            *both(levels, 2, col_count),
-            *both(levels),
-            dma((levels, col_count)), dma((levels,)),
-            dma((2, levels, 2, col_count // 2)), dma((2, levels, 2)), dma((2, levels, 2)),
-            *both(levels, 2),
-            *both(2, col_count), *both(3, levels),
-            dma((3, col_count)), dma((3,)),
-            *both(1), *both(levels),
-            dma((2, col_tiles)), dma((col_tiles,)),
-            *both(1),
-        ],
+        scratch_shapes=scratch,
         compiler_params=pltpu.CompilerParams(
-            collective_id=0, has_side_effects=True, vmem_limit_bytes=60 * 1024 * 1024
+            collective_id=0, has_side_effects=True, vmem_limit_bytes=held + 4 * half * full + 4 * 1024 * 1024
         ),
         cost_estimate=pl.CostEstimate(
             flops=400_000_000, bytes_accessed=4_000_000, transcendentals=0
@@ -888,22 +966,30 @@
     moves = [spin, first]
     high, middle, low = parts_of(left[...])
     lhs = jnp.concatenate([high, high, middle, middle, high, low], axis=0).astype(BF16)
-    for parity in range(2):
-        other = right[parity]
+    sides = []
+    for side in range(2):
+        other = right[side]
         other = jnp.concatenate([other[PB:], other[:PB]], axis=0)
         high, middle, low = parts_of(other)
-        rhs = jnp.concatenate([high, middle, high, middle, low, high], axis=0).astype(BF16)
-        width = row_tiles * tile
-        at = parity * width
-        updated[:, at : at + width] = reduced[:, at : at + width] - inner(lhs, rhs)
-        for t in range(row_tiles):
-            position = parity * row_tiles + t
-            move = pltpu.make_async_copy(
-                updated.at[:, position * tile : (position + 1) * tile],
-                updated_out.at[:, place(position)], sems.at[2 + position],
-            )
-            move.start()
-            moves.append(move)
+        sides.append(
+            jnp.concatenate([high, middle, high, middle, low, high], axis=0).astype(BF16)
+        )
+    width = row_tiles * tile
+    for block in range(row_tiles):
+        at = block * tile
+        for side in range(2):
+            value = reduced[at : at + tile, side * width : (side + 1) * width] - inner(
+                lhs[:, at : at + tile], sides[side]
+            )
+            for t in range(row_tiles):
+                updated[at : at + tile, place(side * row_tiles + t), :] = (
+                    value[:, t * tile : (t + 1) * tile]
+                )
+        move = pltpu.make_async_copy(
+            updated.at[at : at + tile], updated_out.at[at : at + tile], sems.at[2 + block]
+        )
+        move.start()
+        moves.append(move)
     for move in moves:
         move.wait()
 
@@ -923,9 +1009,10 @@
         in_specs=[whole] * 6,
         out_specs=(hbm, hbm, whole, whole, hbm),
         scratch_shapes=[
-            pltpu.VMEM((row_tiles * tile, col_tiles * tile), F32),
-            pltpu.SemaphoreType.DMA((2 + col_tiles,)),
+            pltpu.VMEM(shape, F32),
+            pltpu.SemaphoreType.DMA((2 + row_tiles,)),
         ],
+        compiler_params=pltpu.CompilerParams(vmem_limit_bytes=16 * 1024 * 1024),
         cost_estimate=pl.CostEstimate(
             flops=200_000_000, bytes_accessed=8_000_000, transcendentals=0
         ),
@@ -940,7 +1027,7 @@
     row_count = lax.axis_size("row")
     col_count = lax.axis_size("col")
     sizes = (row_count, col_count, row_tiles, col_tiles, tile)
-    flat = eigvec.reshape(row_tiles * tile, col_tiles * tile)
+    flat = eigvec.reshape(row_tiles * tile, col_tiles, tile)
     parts = step(psi, hpsi, flat, sizes)
     updated, correlation, diagonal, offdiag, rotated = finish(parts, sizes)
     tile_shape = (row_tiles, 1, tile, col_tiles, 1, tile)

time: 125 us -> 112 us (0.90)
  Pallas kernels: 121 us -> 107 us
    pallas_call x1, Pallas kernels: 116 us -> 105 us  [step(): pl.pallas_call(functools.partial(step_kernel, sizes), out_shape=(jax.Shap...]
    pallas_call x1, Pallas kernels: 4.96 us -> 2.81 us  [finish(): pl.pallas_call(functools.partial(finish_kernel, sizes), out_shape=(jax.Sh...]
    unnamed x1 -> x6, local copies, waits for them, and re-layouts: 2.47 us -> 3.12 us
where the time goes in v4:
time: 112 us; the launch traced here: 111 us
  Pallas kernels  107 us (96%)
  local copies, waits for them, and re-layouts  3.12 us (3%)
    pallas_call x1, Pallas kernels, step(): pl.pallas_call(functools.partial(step_kernel, sizes), out_shape=(jax.Shap...  105 us
    unnamed x6, local copies, waits for them, and re-layouts  3.12 us
    pallas_call x1, Pallas kernels, finish(): pl.pallas_call(functools.partial(finish_kernel, sizes), out_shape=(jax.Sh...  2.81 us

profile of v4, /device:TPU:0, one launch (start us, length us, event | category | flops | bytes accessed | tf_op | source)
XLA Modules:
  0.0 111.2 jit_solution(7348194675715163511)
XLA Ops:
  0.6 0.0 copy-start
  0.6 1.2 %copy-done = bf16[4,1,128,8,1,128]{5,3,4,2,1,0:T(8,128)(2,1)S(1)} copy-done((bf16[4,1,128,8,1,128]{5,3,4,2,1,0:T(8,128)(2,1)S(1)}, bf16[4,1,128,8,1,128]{5,3,4,2,1,0:T(8,128)(2,1)}, u32[]{:S(2)}) %copy-start) | copy-done | bytes 1048600
  1.9 0.0 copy-start.1
  1.9 0.9 copy-done.1
  2.8 0.0 copy-start.2
  2.8 0.9 copy-done.2
  3.8 104.5 %step.1 = (f32[512,1024]{1,0:T(8,128)S(1)}, f32[512,8,128]{2,1,0:T(8,128)S(1)}, f32[32,512]{1,0:T(8,128)S(1)}, f32[2,32,512]{2,1,0:T(8,128)S(1)}, f32[8,128]{1,0...) custom-call(bf16[32,4096]{1,0:T(8,128)(2,1)S(1)} %copy-done.1, bf16[32,4096]{1,0:T(8,128)(2,1)S(1)} %copy-done.2, ...), custom_call_target="tpu_custom_call" | custom-call | flops 400000000 | bytes 4000000 | tf_op jit(solution)/shard_map/step/pallas_call | solution.py:928
  108.3 2.8 %finish.1 = (f32[512,8,128]{2,1,0:T(8,128)}, f32[512,8,128]{2,1,0:T(8,128)}, f32[1,16]{1,0:T(1,128)}, f32[1,16]{1,0:T(1,128)}, bf16[128,8,128]{2,1,0:T(8,128)(2,1)}) custom-call(f32[512,1024]{1,0:T(8,128)S(1)} %get-tuple-element.16.reduced, f32[512,8,128]{2,1,0:T(8,128)S(1)} %get-tuple-element.17.correlation, f32[32,512]{1,0:T(8,128)S(1)} %get-tuple-element.18.left, ...), custom_call_target="tpu_custom_call" | custom-call | flops 200000000 | bytes 8000000 | tf_op jit(solution)/shard_map/finish/pallas_call | solution.py:1002
Async XLA Ops:
  0.6 1.2 %copy-start = (bf16[4,1,128,8,1,128]{5,3,4,2,1,0:T(8,128)(2,1)S(1)}, bf16[4,1,128,8,1,128]{5,3,4,2,1,0:T(8,128)(2,1)}, u32[]{:S(2)}) copy-start(bf16[4,1,128,8,1,128]{5,3,4,2,1,0:T(8,128)(2,1)} %param.5) | copy-start | bytes 3145732
  1.9 0.9 copy-start.1
  2.8 0.9 copy-start.2

commit v5 on v4

--- a/solution.py
+++ b/solution.py
@@ -10,6 +10,7 @@
 
 PB = 16
 LEAD = 32
+LEAD_ROWS = 24
 F32 = jnp.float32
 BF16 = jnp.bfloat16
 MESH = pl.DeviceIdType.MESH
@@ -48,13 +49,13 @@
 
 def step_kernel(
     sizes, psi_in, hpsi_in, eig,
-    reduced, ordered, left, right, ends, rotated,
-    psi, hpsi, col_all, row_all, lead_all, stage, natural, turned, panel, partial, vw,
-    message, outgoing, zmessage, zoutgoing, eig_raw, eig_flat, keep, inbox, spun, spun_other,
+    reduced_out, ordered_out, left, right, ends, rotated,
+    reduced, ordered, psi, hpsi, col_all, row_all, lead_all, stage, natural, turned, panel, partial, vw,
+    message, outgoing, zmessage, zoutgoing, lead_rows, eig_raw, eig_flat, keep, inbox, spun, spun_other,
     s1_send, s1_recv, up_send, up_recv, down_send, down_recv, sib_send, sib_recv,
     leadz_send, leadz_recv, leadp_send, leadp_recv, row_send, row_recv, own_sem,
     give_send, give_recv, msg_send, msg_recv, zmsg_send, zmsg_recv,
-    end_send, end_recv, eig_send, eig_recv, upsum_send, upsum_recv, downsum_send, downsum_recv, load_sem,
+    end_send, end_recv, eig_send, eig_recv, upsum_send, upsum_recv, downsum_send, downsum_recv, load_sem, leave_sem,
     spin_send, spin_recv,
 ):
     row_count, col_count, row_tiles, col_tiles, tile = sizes
@@ -163,6 +164,12 @@
             reduced[pl.ds(at, tile), side * half : (side + 1) * half] = 0.5 * (
                 inner(rows_of(0), cols_of(1)) + inner(rows_of(1), cols_of(0))
             )
+
+    def leave():
+        return [
+            pltpu.make_async_copy(reduced, reduced_out, leave_sem.at[0]),
+            pltpu.make_async_copy(ordered, ordered_out, leave_sem.at[1]),
+        ]
 
     def helper_core():
         not_top = z < levels - 1
@@ -398,6 +405,9 @@
         def _(index):
             block_work(index, 0)
 
+        for copy in leave():
+            copy.start()
+
         def pass_up(high):
             @pl.when(jnp.logical_and(z > 0, z < high))
             def _():
@@ -483,6 +493,8 @@
                 downsum(level, level).wait_send()
 
         spin_give().wait_send()
+        for copy in leave():
+            copy.wait()
         left_in().wait_recv()
         right_copy().wait_recv()
         ends_copy().wait_recv()
@@ -764,8 +776,15 @@
         for level in range(1, levels):
             start = start + lead_product(level)
         panel[...] = start
-
-        rows_at = EARLY + 4
+        for level in range(levels):
+            for kk in range(2):
+                for a in range(2):
+                    at = a * gvecs + (level * 2 + kk) * deep
+                    lead_rows[:, at : at + deep] = (
+                        0.5 * lead_all[level, kk, 1 - a].astype(F32)[:LEAD_ROWS]
+                    )
+
+        rows_at = EARLY + 3
         work_at = rows_at + 1
 
         def background(step):
@@ -778,6 +797,11 @@
             @pl.when(jnp.logical_and(step >= work_at, step < work_at + row_tiles))
             def _():
                 block_work(step - work_at, 1)
+
+            @pl.when(step == work_at + row_tiles)
+            def _():
+                for copy in leave():
+                    copy.start()
 
         @pl.loop(EARLY, PB)
         def _(step):
@@ -801,10 +825,15 @@
             sums = received[:, : 2 * gvecs]
             pieces = pieces_of(sums)
             product = 0.5 * rows_sum(
-                jnp.dot(pieces[:, :gvecs], natural[1], preferred_element_type=F32)
-                + jnp.dot(pieces[:, gvecs:], natural[0], preferred_element_type=F32)
+                jnp.dot(pieces[:, :gvecs], natural[1, :, :full], preferred_element_type=F32)
+                + jnp.dot(pieces[:, gvecs:], natural[0, :, :full], preferred_element_type=F32)
             )
             whole_sum = rows_sum(sums)
+            edge_rows = lanes_sum(lead_rows[...] * whole_sum)
+            edge_rows = rows_sum(
+                jnp.where(lane2[:LEAD_ROWS] == sub2[:LEAD_ROWS], edge_rows, 0.0)
+            )
+            product = jnp.concatenate([product, edge_rows], axis=1)
             square = lanes_sum(whole_sum[:, :gvecs] * whole_sum[:, gvecs:])
             settle(step, both, column, product, square, rows_sum(received[:, 2 * gvecs :]))
 
@@ -840,6 +869,8 @@
         def _():
             left_in().wait_recv()
 
+        for copy in leave():
+            copy.wait()
         each_left(lambda copy: copy.wait_send())
         right_copy().wait_send()
         ends_copy().wait_send()
@@ -887,6 +918,8 @@
         return [dma(shape), dma(shape)]
 
     scratch = [
+        pltpu.VMEM((half, full), F32),
+        pltpu.VMEM((half, col_tiles, tile), F32),
         pltpu.VMEM((g_rows, psi.shape[1]), BF16),
         pltpu.VMEM((g_rows, psi.shape[1]), BF16),
         pltpu.VMEM((2, levels, 2, col_count, g_rows, full), BF16),
@@ -902,6 +935,7 @@
         pltpu.VMEM((2, 8, 2 * gvecs + tile), F32),
         pltpu.VMEM((3, 8, 2 * wide + tile), F32),
         pltpu.VMEM((3, 8, 2 * wide + tile), F32),
+        pltpu.VMEM((LEAD_ROWS, 2 * gvecs), F32),
         pltpu.VMEM((2, half, col_tiles, tile), BF16),
         pltpu.VMEM((2, half, full), BF16),
         pltpu.VMEM((levels, 2 * deep, full), F32),
@@ -918,7 +952,7 @@
         *both(levels, 2),
         *both(2, col_count), *both(3, levels),
         dma((3, col_count)), dma((3,)),
-        *both(1), *both(levels), *both(levels), dma((2,)),
+        *both(1), *both(levels), *both(levels), dma((2,)), dma((2,)),
         *both(1),
     ]
     held = sum(
@@ -936,7 +970,7 @@
             jax.ShapeDtypeStruct((deep, col_tiles, tile), BF16),
         ),
         in_specs=[pl.BlockSpec(memory_space=pltpu.HBM)] * 3,
-        out_specs=(whole,) * 6,
+        out_specs=(pl.BlockSpec(memory_space=pl.ANY),) * 2 + (whole,) * 4,
         scratch_shapes=scratch,
         compiler_params=pltpu.CompilerParams(
             collective_id=0, has_side_effects=True, vmem_limit_bytes=held + 4 * half * full + 4 * 1024 * 1024
@@ -1006,7 +1040,7 @@
             jax.ShapeDtypeStruct((1, PB), F32), jax.ShapeDtypeStruct((1, PB), F32),
             jax.ShapeDtypeStruct(parts[-1].shape, BF16),
         ),
-        in_specs=[whole] * 6,
+        in_specs=[whole, hbm, whole, whole, whole, hbm],
         out_specs=(hbm, hbm, whole, whole, hbm),
         scratch_shapes=[
             pltpu.VMEM(shape, F32),

time: 112 us -> 111 us (level)
  no operation moved by 1% of the time
where the time goes in v5:
time: 111 us
  Pallas kernels  107 us (96%)
  local copies, waits for them, and re-layouts  3.12 us (3%)
    pallas_call x1, Pallas kernels, step(): pl.pallas_call(functools.partial(step_kernel, sizes), out_shape=(jax.Shap...  105 us
    unnamed x6, local copies, waits for them, and re-layouts  3.12 us
    pallas_call x1, Pallas kernels, finish(): pl.pallas_call(functools.partial(finish_kernel, sizes), out_shape=(jax.Sh...  2.8 us

profile of v5, /device:TPU:0, one launch (start us, length us, event | category | flops | bytes accessed | tf_op | source)
XLA Modules:
  0.0 111.3 jit_solution(9398836100368124930)
XLA Ops:
  0.6 0.0 copy-start
  0.6 1.2 %copy-done = bf16[4,1,128,8,1,128]{5,3,4,2,1,0:T(8,128)(2,1)S(1)} copy-done((bf16[4,1,128,8,1,128]{5,3,4,2,1,0:T(8,128)(2,1)S(1)}, bf16[4,1,128,8,1,128]{5,3,4,2,1,0:T(8,128)(2,1)}, u32[]{:S(2)}) %copy-start) | copy-done | bytes 1048600
  1.9 0.0 copy-start.1
  1.9 0.9 copy-done.1
  2.8 0.0 copy-start.2
  2.8 0.9 copy-done.2
  3.8 104.5 %step.1 = (f32[512,1024]{1,0:T(8,128)S(1)}, f32[512,8,128]{2,1,0:T(8,128)S(1)}, f32[32,512]{1,0:T(8,128)S(1)}, f32[2,32,512]{2,1,0:T(8,128)S(1)}, f32[8,128]{1,0...) custom-call(bf16[32,4096]{1,0:T(8,128)(2,1)S(1)} %copy-done.1, bf16[32,4096]{1,0:T(8,128)(2,1)S(1)} %copy-done.2, ...), custom_call_target="tpu_custom_call" | custom-call | flops 400000000 | bytes 4000000 | tf_op jit(solution)/shard_map/step/pallas_call | solution.py:962
  108.3 2.8 %finish.1 = (f32[512,8,128]{2,1,0:T(8,128)}, f32[512,8,128]{2,1,0:T(8,128)}, f32[1,16]{1,0:T(1,128)}, f32[1,16]{1,0:T(1,128)}, bf16[128,8,128]{2,1,0:T(8,128)(2,1)}) custom-call(f32[512,1024]{1,0:T(8,128)S(1)} %get-tuple-element.16.reduced, f32[512,8,128]{2,1,0:T(8,128)S(1)} %get-tuple-element.17.correlation, f32[32,512]{1,0:T(8,128)S(1)} %get-tuple-element.18.left, ...), custom_call_target="tpu_custom_call" | custom-call | flops 200000000 | bytes 8000000 | tf_op jit(solution)/shard_map/finish/pallas_call | solution.py:1036
Async XLA Ops:
  0.6 1.2 %copy-start = (bf16[4,1,128,8,1,128]{5,3,4,2,1,0:T(8,128)(2,1)S(1)}, bf16[4,1,128,8,1,128]{5,3,4,2,1,0:T(8,128)(2,1)}, u32[]{:S(2)}) copy-start(bf16[4,1,128,8,1,128]{5,3,4,2,1,0:T(8,128)(2,1)} %param.5) | copy-start | bytes 3145732
  1.9 0.9 copy-start.1
  2.8 0.9 copy-start.2
